TPU v7x, 8 devices: a whole 2x2x1 slice. The times are simulated.
8 devices in a mesh: problem: 1 (over z), samp: 2 (over y), feat: 4 (over x, core).
Axes of the slice: x: 2, y: 2, z: 1, core: 2. Of those that a mesh axis runs over, the one named last changes fastest.
Arguments:
- design: bfloat16 [4096, 131072], P(('problem', 'samp'), 'feat')
- targets: float32 [4096, 128], P(('problem', 'samp'))
- coef_init: float32 [131072, 128], P(('problem', 'feat'))
- step_sizes: float32 [131072], P(('problem', 'feat'))
- ridge_weights: float32 [128], P('problem')
Outputs:
- output 1: float32 [131072, 128], P(('problem', 'feat'))
- output 2: float32 [4096, 128], P(('problem', 'samp'))
All inputs are finite; a program needn't handle non-finite values.
Results may differ from a plain program's by a relative error of at most 0.00677784.
Values are sent between devices in bfloat16 or wider.
A program may use at most 1 GiB of HBM per device.

v0:
```python
import jax
import jax.numpy as jnp
from jax import lax
from jax.sharding import PartitionSpec as P

SWEEPS = 4
STEP_WEIGHT = 0.5


def solution(mesh):
    samp_size = mesh.shape["samp"]
    design_spec = P(("problem", "samp"), "feat")
    rows_spec = P(("problem", "samp"), None)
    coef_spec = P(("problem", "feat"), None)
    step_spec = P(("problem", "feat"))
    ridge_spec = P("problem")

    def local_sweeps(design, targets, coef_init, step_sizes, ridge_weights):
        total_rows = design.shape[0] * samp_size
        step_col = step_sizes[:, None]
        ridge_row = ridge_weights[None, :]

        def block_product(weights):
            product = jnp.dot(design, weights.astype(jnp.bfloat16), preferred_element_type=jnp.float32)
            return product.astype(jnp.bfloat16).astype(jnp.float32)

        resid_cur = targets - lax.psum(block_product(coef_init), "feat")
        coef_cur = coef_init
        for sweep_index in range(SWEEPS):
            part_grad = lax.dot_general(design, resid_cur.astype(jnp.bfloat16), (((0,), (0,)), ((), ())), preferred_element_type=jnp.float32)
            gradient = lax.psum(part_grad, "samp") / total_rows
            step_delta = step_col * (gradient - ridge_row * coef_cur)
            coef_cur = coef_cur + STEP_WEIGHT * step_delta
            resid_cur = resid_cur - STEP_WEIGHT * lax.psum(block_product(step_delta), "feat")
        return coef_cur, resid_cur

    return jax.shard_map(local_sweeps, mesh=mesh, in_specs=(design_spec, rows_spec, coef_spec, step_spec, ridge_spec), out_specs=(coef_spec, rows_spec), check_vma=False)
```

profile of v0, /device:TPU:0, one launch (start us, length us, event | category | flops | bytes accessed | tf_op | source)
XLA Modules:
  0.0 2156.2 jit_solution(7951827969665737439)
XLA Ops:
  7.2 0.0 copy-start.3
  7.2 0.0 all-reduce.10.cloned.1.call-start
  7.2 51.9 %fusion.29 = f32[2048,128]{1,0:T(8,128)} fusion(bf16[2048,32768]{1,0:T(8,128)(2,1)} %param.5, f32[32768,128]{1,0:T(8,128)} %param.7), kind=kOutput, calls=%fused_computation.35 | convolution fusion | flops 17184587776 | bytes 152043520 | tf_op jit(solution)/shard_map/dot_general | solution.py:24
  59.1 0.0 all-reduce.10.cloned.1.call-update
  59.2 0.0 all-reduce.12.cloned.1.call-start
  59.2 33.8 %all-reduce.10.cloned.1.call-done = f32[2048,128]{1,0:T(8,128)} async-done(((f32[2048,128]{1,0:T(8,128)}), f32[2048,128]{1,0:T(8,128)}) %all-reduce.10.cloned.1.call-update) | async-done | bytes 1048592 | tf_op jit(solution)/shard_map/psum | solution.py:27
  93.0 0.0 copy-done.3
  93.0 1.3 sub.27
  94.3 49.4 %convolution_bitcast_fusion.3 = f32[32768,128]{0,1:T(8,128)} fusion(bf16[2048,32768]{1,0:T(8,128)(2,1)} %param.5, f32[2048,128]{1,0:T(8,128)S(1)} %sub.27), kind=kOutput, calls=%fused_computation.3 | convolution fusion | flops 17180131328 | bytes 152043520 | tf_op jit(solution)/shard_map/dot_general | solution.py:30
  143.7 0.0 all-reduce.12.cloned.1.call-update
  143.8 0.0 copy-start
  143.8 0.0 copy-start.4
  143.8 0.2 all-reduce.14.cloned.1.call-start
  144.0 17.4 copy.8
  161.5 354.9 %all-reduce.12.cloned.1.call-done = f32[32768,128]{0,1:T(8,128)} async-done(((f32[32768,128]{0,1:T(8,128)}), f32[32768,128]{0,1:T(8,128)}) %all-reduce.12.cloned.1.call-update) | async-done | bytes 16777232 | tf_op jit(solution)/shard_map/psum | solution.py:31
  516.3 0.0 copy-done
  516.3 54.4 %fusion.38 = f32[2048,128]{1,0:T(8,128)} fusion(bf16[2048,32768]{1,0:T(8,128)(2,1)} %param.5, f32[32768,128]{0,1:T(8,128)} %copy.8, f32[32768,128]{0,1:T(8,128)} %all-reduce.12.cloned.1.call-done, f32[128]{0:T(128)S(1)} %copy-done.4, f32[32768]{0:T(1024)S(1)} %copy-done), kind=kOutput, calls=%fused_computation.38 | convolution fusion | flops 17201364992 | bytes 168952320 | tf_op jit(solution)/shard_map/dot_general | solution.py:24
  570.8 0.0 all-reduce.14.cloned.1.call-update
  570.8 0.0 all-reduce.16.cloned.1.call-start
  570.8 31.3 %all-reduce.14.cloned.1.call-done = f32[2048,128]{1,0:T(8,128)} async-done(((f32[2048,128]{1,0:T(8,128)}), f32[2048,128]{1,0:T(8,128)}) %all-reduce.14.cloned.1.call-update) | async-done | bytes 1048592 | tf_op jit(solution)/shard_map/psum | solution.py:34
  602.1 49.7 %convolution_bitcast_fusion.2 = f32[32768,128]{0,1:T(8,128)} fusion(bf16[2048,32768]{1,0:T(8,128)(2,1)} %param.5, f32[2048,128]{1,0:T(8,128)S(1)} %sub.27, f32[2048,128]{1,0:T(8,128)} %all-reduce.14.cloned.1.call-done), kind=kOutput, calls=%fused_computation.2 | convolution fusion | flops 17180655616 | bytes 153092096 | tf_op jit(solution)/shard_map/dot_general | solution.py:30
  651.8 0.0 all-reduce.16.cloned.1.call-update
  651.8 0.0 all-reduce.18.cloned.1.call-start
  651.9 372.5 %all-reduce.16.cloned.1.call-done = f32[32768,128]{0,1:T(8,128)} async-done(((f32[32768,128]{0,1:T(8,128)}), f32[32768,128]{0,1:T(8,128)}) %all-reduce.16.cloned.1.call-update) | async-done | bytes 16777232 | tf_op jit(solution)/shard_map/psum | solution.py:31
  1024.4 59.2 %fusion.47 = f32[2048,128]{1,0:T(8,128)} fusion(bf16[2048,32768]{1,0:T(8,128)(2,1)} %param.5, f32[32768,128]{0,1:T(8,128)} %all-reduce.16.cloned.1.call-done, f32[128]{0:T(128)S(1)} %copy-done.4, f32[32768]{0:T(1024)S(1)} %copy-done, f32[32768,128]{0,1:T(8,128)} %copy.8, f32[32768,128]{0,1:T(8,128)} %all-reduce.12.cloned.1.call-done), kind=kOutput, calls=%fused_computation.41 | convolution fusion | flops 17226530816 | bytes 185729536 | tf_op jit(solution)/shard_map/dot_general | solution.py:24
  1083.6 0.0 all-reduce.18.cloned.1.call-update
  1083.6 0.3 all-reduce.20.cloned.1.call-start
  1083.9 31.1 %all-reduce.18.cloned.1.call-done = f32[2048,128]{1,0:T(8,128)} async-done(((f32[2048,128]{1,0:T(8,128)}), f32[2048,128]{1,0:T(8,128)}) %all-reduce.18.cloned.1.call-update) | async-done | bytes 1048592 | tf_op jit(solution)/shard_map/psum | solution.py:34
  1115.0 1.4 multiply_subtract_fusion.2
  1116.3 49.5 %convolution_bitcast_fusion.1 = f32[32768,128]{0,1:T(8,128)} fusion(bf16[2048,32768]{1,0:T(8,128)(2,1)} %param.5, f32[2048,128]{1,0:T(8,128)S(1)} %multiply_subtract_fusion.2), kind=kOutput, calls=%fused_computation.1 | convolution fusion | flops 17180131328 | bytes 152043520 | tf_op jit(solution)/shard_map/dot_general | solution.py:30
  1165.8 0.0 all-reduce.20.cloned.1.call-update
  1165.8 0.0 all-reduce.22.cloned.1.call-start
  1165.9 23.8 %multiply_add_fusion.2 = f32[32768,128]{0,1:T(8,128)} fusion(f32[32768,128]{0,1:T(8,128)} %all-reduce.16.cloned.1.call-done, f32[128]{0:T(128)S(1)} %copy-done.4, f32[32768]{0:T(1024)S(1)} %copy-done, f32[32768,128]{0,1:T(8,128)} %copy.8, f32[32768,128]{0,1:T(8,128)} %all-reduce.12.cloned.1.call-done), kind=kLoop, calls=%fused_computation.8 | loop fusion | flops 50331648 | bytes 67240448 | tf_op jit(solution)/shard_map/add | solution.py:33
  1189.7 348.7 %all-reduce.20.cloned.1.call-done = f32[32768,128]{0,1:T(8,128)} async-done(((f32[32768,128]{0,1:T(8,128)}), f32[32768,128]{0,1:T(8,128)}) %all-reduce.20.cloned.1.call-update) | async-done | bytes 16777232 | tf_op jit(solution)/shard_map/psum | solution.py:31
  1538.4 54.5 %fusion.56 = f32[2048,128]{1,0:T(8,128)} fusion(bf16[2048,32768]{1,0:T(8,128)(2,1)} %param.5, f32[32768,128]{0,1:T(8,128)} %multiply_add_fusion.2, f32[32768,128]{0,1:T(8,128)} %all-reduce.20.cloned.1.call-done, f32[128]{0:T(128)S(1)} %copy-done.4, f32[32768]{0:T(1024)S(1)} %copy-done), kind=kOutput, calls=%fused_computation.44 | convolution fusion | flops 17201364992 | bytes 168952320 | tf_op jit(solution)/shard_map/dot_general | solution.py:24
  1592.9 0.0 all-reduce.22.cloned.1.call-update
  1592.9 0.3 all-reduce.24.cloned.1.call-start
  1593.2 31.0 %all-reduce.22.cloned.1.call-done = f32[2048,128]{1,0:T(8,128)} async-done(((f32[2048,128]{1,0:T(8,128)}), f32[2048,128]{1,0:T(8,128)}) %all-reduce.22.cloned.1.call-update) | async-done | bytes 1048592 | tf_op jit(solution)/shard_map/psum | solution.py:34
  1624.2 49.6 %convolution_bitcast_fusion = f32[32768,128]{0,1:T(8,128)} fusion(bf16[2048,32768]{1,0:T(8,128)(2,1)} %param.5, f32[2048,128]{1,0:T(8,128)S(1)} %multiply_subtract_fusion.2, f32[2048,128]{1,0:T(8,128)} %all-reduce.22.cloned.1.call-done), kind=kOutput, calls=%fused_computation | convolution fusion | flops 17180655616 | bytes 153092096 | tf_op jit(solution)/shard_map/dot_general | solution.py:30
  1673.9 0.0 all-reduce.24.cloned.1.call-update
  1673.9 0.0 all-reduce.26.cloned.1.call-start
  1673.9 372.5 %all-reduce.24.cloned.1.call-done = f32[32768,128]{0,1:T(8,128)} async-done(((f32[32768,128]{0,1:T(8,128)}), f32[32768,128]{0,1:T(8,128)}) %all-reduce.24.cloned.1.call-update) | async-done | bytes 16777232 | tf_op jit(solution)/shard_map/psum | solution.py:31
  2046.5 59.2 %fusion.65 = f32[2048,128]{1,0:T(8,128)} fusion(bf16[2048,32768]{1,0:T(8,128)(2,1)} %param.5, f32[32768,128]{0,1:T(8,128)} %all-reduce.24.cloned.1.call-done, f32[128]{0:T(128)S(1)} %copy-done.4, f32[32768]{0:T(1024)S(1)} %copy-done, f32[32768,128]{0,1:T(8,128)} %multiply_add_fusion.2, f32[32768,128]{0,1:T(8,128)} %all-reduce.20.cloned.1.call-done), kind=kOutput, calls=%fused_computation.47 | convolution fusion | flops 17226530816 | bytes 185729536 | tf_op jit(solution)/shard_map/dot_general | solution.py:24
  2105.7 0.0 all-reduce.26.cloned.1.call-update
  2105.7 23.7 %multiply_add_fusion = f32[32768,128]{0,1:T(8,128)} fusion(f32[32768,128]{0,1:T(8,128)} %all-reduce.24.cloned.1.call-done, f32[128]{0:T(128)S(1)} %copy-done.4, f32[32768]{0:T(1024)S(1)} %copy-done, f32[32768,128]{0,1:T(8,128)} %multiply_add_fusion.2, f32[32768,128]{0,1:T(8,128)} %all-reduce.20.cloned.1.call-done), kind=kLoop, calls=%fused_computation.4 | loop fusion | flops 50331648 | bytes 67240448 | tf_op jit(solution)/shard_map/add | solution.py:33
  2129.4 17.5 copy.13
  2146.9 0.0 copy-done.1
  2146.9 2.3 multiply_subtract_fusion
  (5 shorter events, 0.0 us)
Async XLA Ops:
  7.2 85.8 %copy-start.3 = (f32[2048,128]{1,0:T(8,128)S(1)}, f32[2048,128]{1,0:T(8,128)}, u32[]{:S(2)}) copy-start(f32[2048,128]{1,0:T(8,128)} %param.6) | copy-start | bytes 3145732
  7.2 85.8 %all-reduce.10.cloned.1.call-start = ((), (), s32[]{:S(2)}) async-start(), calls=%async_computation | async-start | bytes 2097152 | tf_op jit(solution)/shard_map/psum | solution.py:27
  59.2 457.2 %all-reduce.12.cloned.1.call-start = ((), (), s32[]{:S(2)}) async-start(), calls=%async_computation.1 | async-start | bytes 33554432 | tf_op jit(solution)/shard_map/psum | solution.py:31
  143.8 372.6 %copy-start = (f32[32768]{0:T(1024)S(1)}, f32[32768]{0:T(1024)}, u32[]{:S(2)}) copy-start(f32[32768]{0:T(1024)} %param.8) | copy-start | bytes 393220
  143.8 372.6 %copy-start.4 = (f32[128]{0:T(128)S(1)}, f32[128]{0:T(128)}, u32[]{:S(2)}) copy-start(f32[128]{0:T(128)} %param.9) | copy-start | bytes 1540
  143.8 458.3 %all-reduce.14.cloned.1.call-start = ((), (), s32[]{:S(2)}) async-start(), calls=%async_computation.2 | async-start | bytes 2097152 | tf_op jit(solution)/shard_map/psum | solution.py:34
  570.8 453.6 %all-reduce.16.cloned.1.call-start = ((), (), s32[]{:S(2)}) async-start(), calls=%async_computation.3 | async-start | bytes 33554432 | tf_op jit(solution)/shard_map/psum | solution.py:31
  651.8 463.1 %copy-start.2 = (f32[2048,128]{1,0:T(8,128)S(1)}, f32[2048,128]{1,0:T(8,128)}, u32[]{:S(2)}) copy-start(f32[2048,128]{1,0:T(8,128)} %all-reduce.14.cloned.1.call-done) | copy-start | bytes 3145732
  651.8 463.1 %all-reduce.18.cloned.1.call-start = ((), (), s32[]{:S(2)}) async-start(), calls=%async_computation.4 | async-start | bytes 2097152 | tf_op jit(solution)/shard_map/psum | solution.py:34
  1083.6 454.8 %all-reduce.20.cloned.1.call-start = ((), (), s32[]{:S(2)}) async-start(), calls=%async_computation.5 | async-start | bytes 33554432 | tf_op jit(solution)/shard_map/psum | solution.py:31
  1165.8 458.4 %all-reduce.22.cloned.1.call-start = ((), (), s32[]{:S(2)}) async-start(), calls=%async_computation.6 | async-start | bytes 2097152 | tf_op jit(solution)/shard_map/psum | solution.py:34
  1592.9 453.6 %all-reduce.24.cloned.1.call-start = ((), (), s32[]{:S(2)}) async-start(), calls=%async_computation.7 | async-start | bytes 33554432 | tf_op jit(solution)/shard_map/psum | solution.py:31
  1673.9 473.0 %all-reduce.26.cloned.1.call-start = ((), (), s32[]{:S(2)}) async-start(), calls=%async_computation.8 | async-start | bytes 2097152 | tf_op jit(solution)/shard_map/psum | solution.py:34
  2129.4 17.5 copy-start.1
Sparse Core Ops, SparseCore 0:
  59.3 33.6 all-reduce.9
  143.9 372.3 all-reduce.11
  570.9 31.1 all-reduce.13
  651.9 372.4 all-reduce.15
  1083.7 31.1 all-reduce.17
  1166.0 372.4 all-reduce.19
  1593.0 31.1 all-reduce.21
  1674.0 372.4 all-reduce.23
  2105.8 31.1 all-reduce.25
where the time goes:
time: 2160 us
  waiting for transfers between devices  1580 us (73%)
  matrix products  477 us (22%)
  other arithmetic  52.6 us (2%)
  local copies, waits for them, and re-layouts  34.9 us (2%)
    psum x4, waiting for transfers between devices, local_sweeps(): gradient = lax.psum(part_grad, 'samp') / total_rows  1450 us
    dot_general x5, matrix products, block_product(): jnp.dot(design, weights.astype(jnp.bfloat16), preferred_element_type=jnp....  279 us
    dot_general x4, matrix products, local_sweeps(): lax.dot_general(design, resid_cur.astype(jnp.bfloat16), (((0,), (0,)), ((...  198 us
    psum x4, waiting for transfers between devices, local_sweeps(): lax.psum(block_product(step_delta), 'feat')  93.4 us
    add x2, other arithmetic, local_sweeps(): coef_cur = coef_cur + STEP_WEIGHT * step_delta  47.6 us
  transfers between devices with their start and end apart: 9, of which 8 were waited for; matrix products, arithmetic and copies ran while one was open for 4% of the time, Pallas kernels for 0%

commit v1 on v0

v1 whole, which is shorter than its diff:
```python
import functools

import jax
import jax.numpy as jnp
from jax import lax
from jax.experimental import pallas as pl
from jax.experimental.pallas import tpu as pltpu
from jax.sharding import PartitionSpec as P

SWEEPS = 4
STEP_WEIGHT = 0.5
CHUNK = 1024
SLOTS = 4
GROUPS = 2
MESH = pl.DeviceIdType.MESH


def sweep_kernel(
    total_rows, x_hbm, y_ref, w0_hbm, eta_ref, lam_ref, wt_hbm, rt_ref,
    xbuf, w0buf, gsend, grecv, ssend, srecv, wt, ut, rbt, uall,
    x_sem, w0_sem, g_send, g_recv, s_send, s_recv, u_send, u_recv, w_send, w_recv, out_sem,
):
    z, s, f = lax.axis_index("problem"), lax.axis_index("samp"), lax.axis_index("feat")
    chunks = wt.shape[0]
    targets = rt_ref.shape[0]
    per = targets // GROUPS
    core, chip = f % 2, f // 2
    near = chip * 2 + (1 - core)
    far = (1 - chip) * 2 + core
    partner_id = (z, 1 - s, f)
    near_id, far_id = (z, s, near), (z, s, far)
    own, other = s, 1 - s

    barrier = pltpu.get_barrier_semaphore()
    for device in (partner_id, near_id, far_id):
        pl.semaphore_signal(barrier, inc=1, device_id=device, device_id_type=MESH)

    def x_load(half, k):
        start = pl.multiple_of((half * chunks + k) * CHUNK, CHUNK)
        slot = k % SLOTS
        return pltpu.make_async_copy(x_hbm.at[:, pl.ds(start, CHUNK)], xbuf.at[slot], x_sem.at[slot])

    def w0_load(half, k):
        start = pl.multiple_of((half * chunks + k) * CHUNK, CHUNK)
        slot = k % SLOTS
        return pltpu.make_async_copy(w0_hbm.at[pl.ds(start, CHUNK), :], w0buf.at[slot], w0_sem.at[slot])

    def g_copy(g, k):
        return pltpu.make_async_remote_copy(
            src_ref=gsend.at[g, k], dst_ref=grecv.at[g, k], send_sem=g_send.at[g, k], recv_sem=g_recv.at[g, k],
            device_id=partner_id, device_id_type=MESH)

    def s_copy(g, k):
        return pltpu.make_async_remote_copy(
            src_ref=ssend.at[g, k], dst_ref=srecv.at[g, k], send_sem=s_send.at[g, k], recv_sem=s_recv.at[g, k],
            device_id=partner_id, device_id_type=MESH)

    def w_copy(half, k):
        return pltpu.make_async_remote_copy(
            src_ref=wt.at[k], dst_ref=wt_hbm.at[half * chunks + k], send_sem=w_send.at[k], recv_sem=w_recv.at[k],
            device_id=partner_id, device_id_type=MESH)

    def w_store(k):
        return pltpu.make_async_copy(wt.at[k], wt_hbm.at[own * chunks + k], out_sem.at[k])

    def u_copy(parity, g, slot, which, device):
        return pltpu.make_async_remote_copy(
            src_ref=uall.at[parity, g, slot], dst_ref=uall.at[parity, g, slot],
            send_sem=u_send.at[parity, g, which], recv_sem=u_recv.at[parity, g, which],
            device_id=device, device_id_type=MESH)

    def rows_of(g):
        return pl.ds(g * per, per)

    ahead = SLOTS - 1

    def steps(body, half, next_half=None, more=None):
        def step(k, carry):
            upcoming = k + ahead

            @pl.when(upcoming < chunks)
            def _():
                x_load(half, upcoming).start()

            if next_half is not None:
                wanted = upcoming >= chunks
                if more is not None:
                    wanted = jnp.logical_and(wanted, more)

                @pl.when(wanted)
                def _():
                    x_load(next_half, upcoming - chunks).start()

            x_load(half, k).wait()
            body(k, k % SLOTS)
            return carry

        lax.fori_loop(0, chunks, step, 0)

    for k in range(ahead):
        x_load(own, k).start()
        w0_load(own, k).start()
    ut[...] = jnp.zeros_like(ut)

    def start_half(half, next_half, keep):
        def body(k, slot):
            upcoming = k + ahead

            @pl.when(upcoming < chunks)
            def _():
                w0_load(half, upcoming).start()

            if keep:

                @pl.when(upcoming >= chunks)
                def _():
                    w0_load(next_half, upcoming - chunks).start()

            w0_load(half, k).wait()
            start_t = w0buf[slot].T
            if keep:
                wt[k] = start_t
            ut[...] += lax.dot_general(
                start_t.astype(jnp.bfloat16), xbuf[slot], (((1,), (1,)), ((), ())), preferred_element_type=jnp.float32)

        steps(body, half, next_half)

    start_half(own, other, True)
    rt_ref[...] = y_ref[...].T
    start_half(other, other, False)
    pl.semaphore_wait(barrier, 3)

    def u_begin(parity, g):
        uall[parity, g, f] = ut[rows_of(g), :].astype(jnp.bfloat16)
        ut[rows_of(g), :] = jnp.zeros((per, ut.shape[1]), jnp.float32)
        u_copy(parity, g, f, 0, near_id).start()
        u_copy(parity, g, f, 1, far_id).start()

    def u_end(parity, g, weight):
        u_copy(parity, g, far, 1, far_id).wait_recv()
        u_copy(parity, g, far, 2, near_id).start()
        u_copy(parity, g, near, 0, near_id).wait_recv()
        u_copy(parity, g, far, 2, near_id).wait_recv()
        total = uall[parity, g, 0].astype(jnp.float32)
        for block in range(1, 4):
            total += uall[parity, g, block].astype(jnp.float32)
        new = rt_ref[rows_of(g), :] - (total if weight is None else weight * total)
        rt_ref[rows_of(g), :] = new
        rbt[rows_of(g), :] = new.astype(jnp.bfloat16)
        u_copy(parity, g, f, 0, near_id).wait_send()
        u_copy(parity, g, f, 1, far_id).wait_send()
        u_copy(parity, g, far, 2, near_id).wait_send()

    def partner_gradient(g, next_half):
        def body(k, slot):
            @pl.when(k > 0)
            def _():
                g_copy(g, k - 1).start()

            gsend[g, k] = jnp.dot(rbt[rows_of(g), :], xbuf[slot], preferred_element_type=jnp.float32)

        steps(body, other, next_half)
        g_copy(g, chunks - 1).start()

    def own_columns(g, t, next_half):
        lam = lam_ref[rows_of(g), 0:1]

        def body(k, slot):
            part = jnp.dot(rbt[rows_of(g), :], xbuf[slot], preferred_element_type=jnp.float32)
            g_copy(g, k).wait_recv()

            @pl.when(t > 0)
            def _():
                s_copy(g, k).wait_send()

            weights = wt[k, rows_of(g), :]
            gradient = (part + grecv[g, k]) * (1.0 / total_rows)
            delta = eta_ref[pl.ds(own * chunks + k, 1), :] * (gradient - lam * weights)
            wt[k, rows_of(g), :] = weights + STEP_WEIGHT * delta
            delta_b = delta.astype(jnp.bfloat16)
            ssend[g, k] = delta_b
            ut[rows_of(g), :] += lax.dot_general(
                delta_b, xbuf[slot], (((1,), (1,)), ((), ())), preferred_element_type=jnp.float32)
            s_copy(g, k).start()

        steps(body, own, next_half)

    def partner_columns(g, next_half, more=None):
        def body(k, slot):
            s_copy(g, k).wait_recv()
            g_copy(g, k).wait_send()
            ut[rows_of(g), :] += lax.dot_general(
                srecv[g, k], xbuf[slot], (((1,), (1,)), ((), ())), preferred_element_type=jnp.float32)

        steps(body, other, next_half, more)

    u_begin(0, 0)
    u_begin(0, 1)
    u_end(0, 0, None)
    partner_gradient(0, other)
    u_end(0, 1, None)
    partner_gradient(1, own)

    def sweep(t, carry):
        parity = (t + 1) % 2
        more = t < SWEEPS - 1
        own_columns(0, t, own)
        own_columns(1, t, other)

        @pl.when(t == SWEEPS - 1)
        def _():
            def send(k, inner):
                w_copy(own, k).start()
                w_store(k).start()
                return inner

            lax.fori_loop(0, chunks, send, 0)

        partner_columns(0, other)
        u_begin(parity, 0)
        u_end(parity, 0, STEP_WEIGHT)

        @pl.when(more)
        def _():
            partner_gradient(0, other)

        partner_columns(1, other, more)
        u_begin(parity, 1)
        u_end(parity, 1, STEP_WEIGHT)

        @pl.when(more)
        def _():
            partner_gradient(1, own)

        return carry

    lax.fori_loop(0, SWEEPS, sweep, 0)

    def drain(k, carry):
        for g in range(GROUPS):
            s_copy(g, k).wait_send()
        w_store(k).wait()
        w_copy(own, k).wait_send()
        w_copy(other, k).wait_recv()
        return carry

    lax.fori_loop(0, chunks, drain, 0)


def finish_kernel(wt_ref, rt_ref, w_ref, r_ref):
    w_ref[...] = wt_ref[0].T

    @pl.when(pl.program_id(0) == 0)
    def _():
        r_ref[...] = rt_ref[...].T


def solution(mesh):
    samp_size = mesh.shape["samp"]
    design_spec = P(("problem", "samp"), "feat")
    rows_spec = P(("problem", "samp"), None)
    coef_spec = P(("problem", "feat"), None)
    step_spec = P(("problem", "feat"))
    ridge_spec = P("problem")

    def local_sweeps(design, targets, coef_init, step_sizes, ridge_weights):
        rows, columns = design.shape
        width = targets.shape[1]
        per = width // GROUPS
        chunks = columns // CHUNK // samp_size
        bf16, f32 = jnp.bfloat16, jnp.float32
        vmem, dma = pltpu.VMEM, pltpu.SemaphoreType.DMA
        in_vmem = pl.BlockSpec(memory_space=pltpu.VMEM)
        in_hbm = pl.BlockSpec(memory_space=pltpu.HBM)
        coef_t, resid_t = pl.pallas_call(
            functools.partial(sweep_kernel, rows * samp_size),
            name="sweeps",
            out_shape=(
                jax.ShapeDtypeStruct((columns // CHUNK, width, CHUNK), f32),
                jax.ShapeDtypeStruct((width, rows), f32),
            ),
            in_specs=[in_hbm, in_vmem, in_hbm, in_vmem, in_vmem],
            out_specs=(in_hbm, in_vmem),
            scratch_shapes=[
                vmem((SLOTS, rows, CHUNK), bf16),
                vmem((SLOTS, CHUNK, width), f32),
                vmem((GROUPS, chunks, per, CHUNK), f32),
                vmem((GROUPS, chunks, per, CHUNK), f32),
                vmem((GROUPS, chunks, per, CHUNK), bf16),
                vmem((GROUPS, chunks, per, CHUNK), bf16),
                vmem((chunks, width, CHUNK), f32),
                vmem((width, rows), f32),
                vmem((width, rows), bf16),
                vmem((2, GROUPS, 4, per, rows), bf16),
                dma((SLOTS,)),
                dma((SLOTS,)),
                dma((GROUPS, chunks)),
                dma((GROUPS, chunks)),
                dma((GROUPS, chunks)),
                dma((GROUPS, chunks)),
                dma((2, GROUPS, 3)),
                dma((2, GROUPS, 3)),
                dma((chunks,)),
                dma((chunks,)),
                dma((chunks,)),
            ],
            compiler_params=pltpu.CompilerParams(
                collective_id=0, has_side_effects=True, vmem_limit_bytes=67_000_000),
        )(
            design, targets, coef_init, step_sizes.reshape(columns // CHUNK, CHUNK),
            jnp.broadcast_to(ridge_weights[:, None], (width, 128)),
        )
        return pl.pallas_call(
            finish_kernel,
            name="finish",
            grid=(columns // CHUNK,),
            out_shape=(
                jax.ShapeDtypeStruct((columns, width), f32),
                jax.ShapeDtypeStruct((rows, width), f32),
            ),
            in_specs=[
                pl.BlockSpec((1, width, CHUNK), lambda i: (i, 0, 0)),
                pl.BlockSpec((width, rows), lambda i: (0, 0)),
            ],
            out_specs=(
                pl.BlockSpec((CHUNK, width), lambda i: (i, 0)),
                pl.BlockSpec((rows, width), lambda i: (0, 0)),
            ),
        )(coef_t, resid_t)

    return jax.shard_map(
        local_sweeps, mesh=mesh, in_specs=(design_spec, rows_spec, coef_spec, step_spec, ridge_spec),
        out_specs=(coef_spec, rows_spec), check_vma=False)
```

time: 2160 us -> 1360 us (0.63)
  waiting for transfers between devices: 1580 us -> 0 us
  Pallas kernels: 0 us -> 1360 us
  matrix products: 477 us -> 0 us
  other arithmetic: 52.6 us -> 0 us
  local copies, waits for them, and re-layouts: 34.9 us -> 2.95 us
    psum x9 -> x0, waiting for transfers between devices: 1580 us -> none  [the longest x4 1450 us: local_sweeps(): gradient = lax.psum(part_grad, 'samp') / total_rows]
    pallas_call x0 -> x2, Pallas kernels: none -> 1360 us  [the longest x1 1330 us: local_sweeps(): pl.pallas_call(functools.partial(sweep_kernel, rows * samp_size), name='s...]
    dot_general x9 -> x0, matrix products: 477 us -> none  [the longest x5 279 us: block_product(): jnp.dot(design, weights.astype(jnp.bfloat16), preferred_element_type=jnp....]
    add x2 -> x0, other arithmetic: 47.6 us -> none  [local_sweeps(): coef_cur = coef_cur + STEP_WEIGHT * step_delta]
    unnamed x12 -> x0, local copies, waits for them, and re-layouts: 34.9 us -> none
  transfers between devices with their start and end apart: 9 -> 0, of which waited for: 8 -> 0; matrix products, arithmetic and copies ran while one was open for 4% -> 0% of each run, Pallas kernels for 0% -> 0%
where the time goes in v1:
time: 1360 us
  Pallas kernels  1360 us (100%)
    pallas_call x1, Pallas kernels, local_sweeps(): pl.pallas_call(functools.partial(sweep_kernel, rows * samp_size), name='s...  1330 us

profile of v1, /device:TPU:0, one launch (start us, length us, event | category | flops | bytes accessed | tf_op | source)
XLA Modules:
  0.0 1358.8 jit_solution(39094206725510735)
XLA Ops:
  0.6 1.4 broadcast_in_dim.2.lam_ref
  2.0 1.6 reshape.8.eta_ref
  3.6 1329.3 %sweeps.1 = (f32[32,128,1024]{2,1,0:T(8,128)}, f32[128,2048]{1,0:T(8,128)}) custom-call(bf16[2048,32768]{1,0:T(8,128)(2,1)} %x_hbm.1, f32[2048,128]{1,0:T(8,128)} %y_ref.1, f32[32768,128]{1,0:T(8,128)} %w0_hbm.1, f32[32,1024]{1,0:T(8,128)} %reshape.8.eta_ref, f32[128,128]{1,0:T(8,128)} %broadcast_in_dim.2.lam_ref), custom_call_target="tpu_custom_call" | custom-call | tf_op jit(solution)/shard_map/sweeps/pallas_call | solution.py:275
  1332.9 26.0 %finish.1 = (f32[32768,128]{1,0:T(8,128)}, f32[2048,128]{1,0:T(8,128)}) custom-call(f32[32,128,1024]{2,1,0:T(8,128)} %get-tuple-element.4.wt_ref, f32[128,2048]{1,0:T(8,128)} %get-tuple-element.5.rt_ref), custom_call_target="tpu_custom_call" | custom-call | tf_op jit(solution)/shard_map/finish/pallas_call | solution.py:313

commit v2 on v1

v2 whole, which is shorter than its diff:
```python
import functools

import jax
import jax.numpy as jnp
from jax import lax
from jax.experimental import pallas as pl
from jax.experimental.pallas import tpu as pltpu
from jax.sharding import PartitionSpec as P

SWEEPS = 4
STEP_WEIGHT = 0.5
CHUNK = 1024
SLOTS = 4
GROUPS = ((0, 64), (64, 64))
KEPT = 4
PIECES = (6, 4, 2)
MESH = pl.DeviceIdType.MESH


def dot_t(left, right):
    return lax.dot_general(left, right, (((1,), (1,)), ((), ())), preferred_element_type=jnp.float32)


def sweep_kernel(
    total_rows, x_hbm, y_hbm, w0_hbm, eta_ref, lam_ref,
    r_hbm, w_near, w_far, *rest,
):
    w_pieces, rest = rest[: len(PIECES)], rest[len(PIECES):]
    (
        xbuf, w0buf, rows_buf, gsend, grecv, ssend, srecv, wt, ut, rt, rbt, uall, w0t_a, w0t_b, lam_col,
        x_sem, w0_sem, row_sem, g_send, g_recv, s_send, s_recv, u_send, u_recv, w_send, w_recv, out_sem,
    ) = rest
    z, s, f = lax.axis_index("problem"), lax.axis_index("samp"), lax.axis_index("feat")
    chunks, targets, _ = wt.shape
    core, chip = f % 2, f // 2
    near = chip * 2 + (1 - core)
    far = (1 - chip) * 2 + core
    partner_id = (z, 1 - s, f)
    near_id, far_id = (z, s, near), (z, s, far)
    own, other = s, 1 - s

    barrier = pltpu.get_barrier_semaphore()
    for device in (partner_id, near_id, far_id):
        pl.semaphore_signal(barrier, inc=1, device_id=device, device_id_type=MESH)

    def columns_of(chunk):
        return pl.ds(pl.multiple_of(chunk * CHUNK, CHUNK), CHUNK)

    def x_load(chunk, slot):
        return pltpu.make_async_copy(x_hbm.at[:, columns_of(chunk)], xbuf.at[slot], x_sem.at[slot])

    def w0_load(chunk, slot):
        return pltpu.make_async_copy(w0_hbm.at[columns_of(chunk), :], w0buf.at[slot], w0_sem.at[slot])

    def part(ref, g, k):
        return ref.at[k, pl.ds(*GROUPS[g]), :]

    def rows_of(g):
        return pl.ds(*GROUPS[g])

    def g_copy(g, k):
        return pltpu.make_async_remote_copy(
            src_ref=part(gsend, g, k), dst_ref=part(grecv, g, k), send_sem=g_send.at[g, k], recv_sem=g_recv.at[g, k],
            device_id=partner_id, device_id_type=MESH)

    def s_copy(g, k):
        return pltpu.make_async_remote_copy(
            src_ref=part(ssend, g, k), dst_ref=part(srecv, g, k), send_sem=s_send.at[g, k], recv_sem=s_recv.at[g, k],
            device_id=partner_id, device_id_type=MESH)

    def u_copy(parity, g, slot, which, device):
        rows = uall.at[parity, slot, rows_of(g), :]
        return pltpu.make_async_remote_copy(
            src_ref=rows, dst_ref=rows,
            send_sem=u_send.at[parity, g, which], recv_sem=u_recv.at[parity, g, which],
            device_id=device, device_id_type=MESH)

    ahead = SLOTS - 1

    def steps(body, half, next_half, more=None):
        def step(k, carry):
            upcoming = k + ahead

            @pl.when(upcoming < chunks)
            def _():
                x_load(half * chunks + upcoming, upcoming % SLOTS).start()

            wanted = upcoming >= chunks
            if more is not None:
                wanted = jnp.logical_and(wanted, more)

            @pl.when(wanted)
            def _():
                x_load(next_half * chunks + upcoming - chunks, upcoming % SLOTS).start()

            x_load(half * chunks + k, k % SLOTS).wait()
            body(k, k % SLOTS)
            return carry

        lax.fori_loop(0, chunks, step, 0)

    y_load = pltpu.make_async_copy(y_hbm, rows_buf, row_sem)
    w0_load(0, 0).start()
    for k in range(ahead):
        x_load(k, k).start()
        w0_load(k + 1, (k + 1) % SLOTS).start()
    y_load.start()
    ut[...] = jnp.zeros_like(ut)
    lam_col[...] = jnp.broadcast_to(lam_ref[0:1, :], (targets, targets)).T
    w0_load(0, 0).wait()
    w0t_a[...] = w0buf[0].T.astype(jnp.bfloat16)
    w0_load(4, 0).start()
    y_load.wait()
    rt[...] = rows_buf[...].T
    blocks = 2 * chunks

    def start_pair(pair, carry):
        for odd in range(2):
            now, later = (w0t_b, w0t_a) if odd else (w0t_a, w0t_b)
            chunk = pair * 2 + odd
            slot = chunk % SLOTS
            upcoming = chunk + ahead

            @pl.when(upcoming < blocks)
            def _():
                x_load(upcoming, upcoming % SLOTS).start()

            @pl.when(upcoming >= blocks)
            def _():
                x_load(other * chunks + upcoming - blocks, upcoming % SLOTS).start()

            following = (chunk + 1) % blocks
            w0_load(following, (chunk + 1) % SLOTS).wait()
            x_load(chunk, slot).wait()
            later[...] = w0buf[(chunk + 1) % SLOTS].T.astype(jnp.bfloat16)
            ut[...] += dot_t(now[...], xbuf[slot])
            w0_load((chunk + 5) % blocks, (chunk + 1) % SLOTS).start()
        return carry

    lax.fori_loop(0, chunks, start_pair, 0)
    for k in range(1, 5):
        w0_load(k, k % SLOTS).wait()
    pl.semaphore_wait(barrier, 3)

    def u_begin(parity, g):
        uall[parity, f, rows_of(g), :] = ut[rows_of(g), :].astype(jnp.bfloat16)
        ut[rows_of(g), :] = jnp.zeros((GROUPS[g][1], ut.shape[1]), jnp.float32)
        u_copy(parity, g, f, 0, near_id).start()
        u_copy(parity, g, f, 1, far_id).start()

    def u_end(parity, g, weight):
        u_copy(parity, g, far, 1, far_id).wait_recv()
        u_copy(parity, g, far, 2, near_id).start()
        u_copy(parity, g, near, 0, near_id).wait_recv()
        u_copy(parity, g, far, 2, near_id).wait_recv()
        total = uall[parity, 0, rows_of(g), :].astype(jnp.float32)
        for block in range(1, 4):
            total += uall[parity, block, rows_of(g), :].astype(jnp.float32)
        new = rt[rows_of(g), :] - (total if weight is None else weight * total)
        rt[rows_of(g), :] = new
        rbt[rows_of(g), :] = new.astype(jnp.bfloat16)
        u_copy(parity, g, f, 0, near_id).wait_send()
        u_copy(parity, g, f, 1, far_id).wait_send()
        u_copy(parity, g, far, 2, near_id).wait_send()

    def partner_gradient(g, next_half):
        def body(k, slot):
            @pl.when(k > 0)
            def _():
                g_copy(g, k - 1).start()

            gsend[k, rows_of(g), :] = jnp.dot(rbt[rows_of(g), :], xbuf[slot], preferred_element_type=jnp.float32)

        steps(body, other, next_half)
        g_copy(g, chunks - 1).start()

    def own_columns(g, t, next_half):
        lam = lam_col[rows_of(g), 0:1]

        def body(k, slot):
            mine = jnp.dot(rbt[rows_of(g), :], xbuf[slot], preferred_element_type=jnp.float32)
            g_copy(g, k).wait_recv()

            @pl.when(t > 0)
            def _():
                s_copy(g, k).wait_send()

            weights = wt[k, rows_of(g), :]
            gradient = (mine + grecv[k, rows_of(g), :]) * (1.0 / total_rows)
            delta = eta_ref[0:1, columns_of(own * chunks + k)] * (gradient - lam * weights)
            wt[k, rows_of(g), :] = weights + STEP_WEIGHT * delta
            delta_b = delta.astype(jnp.bfloat16)
            ssend[k, rows_of(g), :] = delta_b
            ut[rows_of(g), :] += dot_t(delta_b, xbuf[slot])
            s_copy(g, k).start()

        steps(body, own, next_half)

    def partner_columns(g, next_half, more=None):
        def body(k, slot):
            s_copy(g, k).wait_recv()
            g_copy(g, k).wait_send()
            ut[rows_of(g), :] += dot_t(srecv[k, rows_of(g), :], xbuf[slot])

        steps(body, other, next_half, more)

    u_begin(0, 0)
    u_begin(0, 1)
    u_end(0, 0, None)
    partner_gradient(0, other)
    u_end(0, 1, None)
    partner_gradient(1, own)

    for k in range(ahead):
        w0_load(own * chunks + k, k).start()

    def keep(k, carry):
        @pl.when(k + ahead < chunks)
        def _():
            w0_load(own * chunks + k + ahead, (k + ahead) % SLOTS).start()

        w0_load(own * chunks + k, k % SLOTS).wait()
        wt[k] = w0buf[k % SLOTS].T
        return carry

    lax.fori_loop(0, chunks, keep, 0)

    def w_store(ref, first, n, k):
        rows = pl.ds(pl.multiple_of(k * CHUNK, CHUNK), CHUNK)
        slot = (first + k) % SLOTS
        return pltpu.make_async_copy(w0buf.at[slot], ref.at[rows, :], out_sem.at[slot])

    def w_copy(k):
        rows = pl.ds(pl.multiple_of(k * CHUNK, CHUNK), CHUNK)
        slot = k % SLOTS
        return pltpu.make_async_remote_copy(
            src_ref=w0buf.at[slot], dst_ref=w_far.at[rows, :], send_sem=w_send.at[slot], recv_sem=w_recv.at[slot],
            device_id=partner_id, device_id_type=MESH)

    def w_out():
        first = 0
        for ref, n in (*zip(w_pieces, PIECES), (w_near, KEPT)):

            def put(k, carry, ref=ref, n=n, first=first):
                chunk = first + k
                slot = chunk % SLOTS

                @pl.when(chunk >= SLOTS)
                def _():
                    w_store(ref, first, n, k).wait()

                w0buf[slot] = wt[chunk].T
                w_store(ref, first, n, k).start()
                return carry

            lax.fori_loop(0, n, put, 0)
            first += n

        def send(k, carry):
            w_copy(k).start()
            return carry

        lax.fori_loop(0, KEPT, send, 0)

    def sweep(t, carry):
        parity = (t + 1) % 2
        more = t < SWEEPS - 1
        own_columns(0, t, own)
        own_columns(1, t, other)

        @pl.when(jnp.logical_not(more))
        def _():
            w_out()

        partner_columns(0, other)
        u_begin(parity, 0)
        u_end(parity, 0, STEP_WEIGHT)

        @pl.when(more)
        def _():
            partner_gradient(0, other)

        partner_columns(1, other, more)
        u_begin(parity, 1)
        u_end(parity, 1, STEP_WEIGHT)

        @pl.when(more)
        def _():
            partner_gradient(1, own)

        return carry

    lax.fori_loop(0, SWEEPS, sweep, 0)
    rows_buf[...] = rt[...].T
    r_store = pltpu.make_async_copy(rows_buf, r_hbm, row_sem)
    r_store.start()

    def drain(k, carry):
        for g in range(len(GROUPS)):
            s_copy(g, k).wait_send()
        return carry

    lax.fori_loop(0, chunks, drain, 0)
    for k in range(KEPT):
        w_store(w_near, sum(PIECES), KEPT, k).wait()
        w_copy(k).wait()
    r_store.wait()


def place(result, piece, half, first, shape):
    rows, width = piece.shape
    halves = shape[0] // CHUNK // 2

    def body(half_ref, piece_ref, *refs):
        refs[-1][...] = piece_ref[...]

    in_specs = [pl.BlockSpec((CHUNK, width), lambda i, half_ref: (i, 0))]
    operands = [piece]
    aliases = {}
    if result is not None:
        in_specs.append(pl.BlockSpec(memory_space=pl.ANY))
        operands.append(result)
        aliases = {2: 0}
    return pl.pallas_call(
        body,
        name="place",
        out_shape=jax.ShapeDtypeStruct(shape, piece.dtype),
        grid_spec=pltpu.PrefetchScalarGridSpec(
            num_scalar_prefetch=1,
            grid=(rows // CHUNK,),
            in_specs=in_specs,
            out_specs=pl.BlockSpec((CHUNK, width), lambda i, half_ref: (half_ref[0] * halves + first + i, 0)),
        ),
        input_output_aliases=aliases,
    )(half, *operands)


def solution(mesh):
    samp_size = mesh.shape["samp"]
    design_spec = P(("problem", "samp"), "feat")
    rows_spec = P(("problem", "samp"), None)
    coef_spec = P(("problem", "feat"), None)
    step_spec = P(("problem", "feat"))
    ridge_spec = P("problem")

    def local_sweeps(design, targets, coef_init, step_sizes, ridge_weights):
        rows, columns = design.shape
        width = targets.shape[1]
        groups = len(GROUPS)
        chunks = columns // CHUNK // samp_size
        bf16, f32 = jnp.bfloat16, jnp.float32
        vmem, dma = pltpu.VMEM, pltpu.SemaphoreType.DMA
        in_vmem = pl.BlockSpec(memory_space=pltpu.VMEM)
        in_hbm = pl.BlockSpec(memory_space=pltpu.HBM)
        sizes = (KEPT, KEPT, *PIECES)
        resid, near, far, *pieces = pl.pallas_call(
            functools.partial(sweep_kernel, rows * samp_size),
            name="sweeps",
            out_shape=(
                jax.ShapeDtypeStruct((rows, width), f32),
                *(jax.ShapeDtypeStruct((n * CHUNK, width), f32) for n in sizes),
            ),
            in_specs=[in_hbm, in_hbm, in_hbm, in_vmem, in_vmem],
            out_specs=(in_hbm,) * (1 + len(sizes)),
            scratch_shapes=[
                vmem((SLOTS, rows, CHUNK), bf16),
                vmem((SLOTS, CHUNK, width), f32),
                vmem((rows, width), f32),
                vmem((chunks, width, CHUNK), f32),
                vmem((chunks, width, CHUNK), f32),
                vmem((chunks, width, CHUNK), bf16),
                vmem((chunks, width, CHUNK), bf16),
                vmem((chunks, width, CHUNK), f32),
                vmem((width, rows), f32),
                vmem((width, rows), f32),
                vmem((width, rows), bf16),
                vmem((2, 4, width, rows), bf16),
                vmem((width, CHUNK), bf16),
                vmem((width, CHUNK), bf16),
                vmem((width, width), f32),
                dma((SLOTS,)),
                dma((SLOTS,)),
                dma,
                dma((groups, chunks)),
                dma((groups, chunks)),
                dma((groups, chunks)),
                dma((groups, chunks)),
                dma((2, groups, 3)),
                dma((2, groups, 3)),
                dma((SLOTS,)),
                dma((SLOTS,)),
                dma((SLOTS,)),
            ],
            compiler_params=pltpu.CompilerParams(
                collective_id=0, has_side_effects=True, vmem_limit_bytes=67_000_000),
        )(design, targets, coef_init, step_sizes.reshape(1, columns), ridge_weights.reshape(1, width))
        here = lax.axis_index("samp").astype(jnp.int32).reshape(1)
        swap = [(i, samp_size - 1 - i) for i in range(samp_size)]
        arrived = [lax.ppermute(piece, "samp", swap) for piece in pieces]
        shape = (columns, width)
        coef = place(None, near, here, sum(PIECES), shape)
        first = 0
        for piece, n in zip(pieces, PIECES):
            coef = place(coef, piece, here, first, shape)
            first += n
        coef = place(coef, far, 1 - here, sum(PIECES), shape)
        first = 0
        for piece, n in zip(arrived, PIECES):
            coef = place(coef, piece, 1 - here, first, shape)
            first += n
        return coef, resid

    return jax.shard_map(
        local_sweeps, mesh=mesh, in_specs=(design_spec, rows_spec, coef_spec, step_spec, ridge_spec),
        out_specs=(coef_spec, rows_spec), check_vma=False)
```

time: 1360 us -> 1340 us (0.985)
  Pallas kernels: 1360 us -> 1220 us
  waiting for transfers between devices: 0 us -> 106 us
    pallas_call x1, Pallas kernels: 1330 us -> 1190 us  [local_sweeps(): pl.pallas_call(functools.partial(sweep_kernel, rows * samp_size), name='s...]
    ppermute x0 -> x3, waiting for transfers between devices: none -> 106 us  [local_sweeps(): arrived = [lax.ppermute(piece, 'samp', swap) for piece in pieces]]
    pallas_call x1 -> x8, Pallas kernels: 26 us -> 29.7 us  [place(): pl.pallas_call(body, name='place', out_shape=jax.ShapeDtypeStruct(shape,...]
  transfers between devices with their start and end apart: 0 -> 3, of which waited for: 0 -> 3; matrix products, arithmetic and copies ran while one was open for 0% -> 0% of each run, Pallas kernels for 0% -> 2%
where the time goes in v2:
time: 1340 us
  Pallas kernels  1220 us (91%)
  waiting for transfers between devices  106 us (8%)
    pallas_call x1, Pallas kernels, local_sweeps(): pl.pallas_call(functools.partial(sweep_kernel, rows * samp_size), name='s...  1190 us
    ppermute x3, waiting for transfers between devices, local_sweeps(): arrived = [lax.ppermute(piece, 'samp', swap) for piece in pieces]  106 us
    pallas_call x8, Pallas kernels, place(): pl.pallas_call(body, name='place', out_shape=jax.ShapeDtypeStruct(shape,...  29.7 us
  transfers between devices with their start and end apart: 3, of which 3 were waited for; matrix products, arithmetic and copies ran while one was open for 0% of the time, Pallas kernels for 2%

profile of v2, /device:TPU:0, one launch (start us, length us, event | category | flops | bytes accessed | tf_op | source)
XLA Modules:
  0.0 1336.1 jit_solution(8041191074372395181)
XLA Ops:
  0.6 1195.0 %sweeps.1 = (f32[2048,128]{1,0:T(8,128)}, f32[4096,128]{1,0:T(8,128)}, f32[4096,128]{1,0:T(8,128)}, f32[6144,128]{1,0:T(8,128)}, f32[4096,128]{1,0:T(8,128)}, /*index=5*/f32[2048,128]{1,0:T(8,128)}) custom-call(bf16[2048,32768]{1,0:T(8,128)(2,1)} %x_hbm.1, f32[2048,128]{1,0:T(8,128)} %y_hbm.1, f32[32768,128]{1,0:T(8,128)} %w0_hbm.1, f32[1,32768]{1,0:T(1,128)} %bitcast.3, ...), custom_call_target="tpu_custom_call" | custom-call | tf_op jit(solution)/shard_map/sweeps/pallas_call | solution.py:356
  1195.6 0.5 collective-permute-start.2
  1196.1 1.5 collective-permute-start.1
  1197.6 0.5 collective-permute-start
  1198.1 3.8 place.8.refs_0_
  1201.9 5.3 place.9.refs_0_
  1207.2 3.8 place.10.refs_0_
  1211.0 2.0 place.11.refs_0_
  1213.0 3.8 place.12.refs_0_
  1216.8 49.8 %collective-permute-done.2.piece_ref = f32[6144,128]{1,0:T(8,128)S(1)} collective-permute-done((f32[6144,128]{1,0:T(8,128)}, f32[6144,128]{1,0:T(8,128)S(1)}, u32[]{:S(2)}, u32[]{:S(2)}) %collective-permute-start.2) | collective-permute-done | bytes 3145760 | tf_op jit(solution)/shard_map/ppermute | solution.py:399
  1266.6 0.0 copy-start
  1266.6 1.7 copy-done
  1268.2 5.3 place.13.refs_0_
  1273.5 38.0 %collective-permute-done.1.piece_ref = f32[4096,128]{1,0:T(8,128)} collective-permute-done((f32[4096,128]{1,0:T(8,128)}, f32[4096,128]{1,0:T(8,128)}, u32[]{:S(2)}, u32[]{:S(2)}) %collective-permute-start.1) | collective-permute-done | bytes 2097184 | tf_op jit(solution)/shard_map/ppermute | solution.py:399
  1311.5 3.8 place.14.refs_0_
  1315.3 0.0 copy-start.1
  1315.3 17.8 %collective-permute-done.piece_ref = f32[2048,128]{1,0:T(8,128)} collective-permute-done((f32[2048,128]{1,0:T(8,128)}, f32[2048,128]{1,0:T(8,128)}, u32[]{:S(2)}, u32[]{:S(2)}) %collective-permute-start) | collective-permute-done | bytes 1048608 | tf_op jit(solution)/shard_map/ppermute | solution.py:399
  1333.1 2.0 place.15
  1335.1 0.0 copy-done.1
  1335.2 1.0 copy.22
Async XLA Ops:
  1195.6 71.0 %collective-permute-start.2 = (f32[6144,128]{1,0:T(8,128)}, f32[6144,128]{1,0:T(8,128)S(1)}, u32[]{:S(2)}, u32[]{:S(2)}) collective-permute-start(f32[6144,128]{1,0:T(8,128)} %get-tuple-element.10.piece_ref), channel_id=1, source_target_pairs={{0,4},{4,0},{1,5},{5,1},{2,6},{6,2},{3,7},{7,3}} | collective-permute-start | bytes 9437192 | tf_op jit(solution)/shard_map/ppermute | solution.py:399
  1196.1 115.4 %collective-permute-start.1 = (f32[4096,128]{1,0:T(8,128)}, f32[4096,128]{1,0:T(8,128)}, u32[]{:S(2)}, u32[]{:S(2)}) collective-permute-start(f32[4096,128]{1,0:T(8,128)} %get-tuple-element.9.piece_ref), channel_id=1, source_target_pairs={{0,4},{4,0},{1,5},{5,1},{2,6},{6,2},{3,7},{7,3}} | collective-permute-start | bytes 6291464 | tf_op jit(solution)/shard_map/ppermute | solution.py:399
  1197.6 135.5 %collective-permute-start = (f32[2048,128]{1,0:T(8,128)}, f32[2048,128]{1,0:T(8,128)}, u32[]{:S(2)}, u32[]{:S(2)}) collective-permute-start(f32[2048,128]{1,0:T(8,128)} %get-tuple-element.8.piece_ref), channel_id=1, source_target_pairs={{0,4},{4,0},{1,5},{5,1},{2,6},{6,2},{3,7},{7,3}} | collective-permute-start | bytes 3145736 | tf_op jit(solution)/shard_map/ppermute | solution.py:399
  1266.6 1.7 copy-start
  1315.3 19.8 %copy-start.1 = (f32[2048,128]{1,0:T(8,128)S(1)}, f32[2048,128]{1,0:T(8,128)}, u32[]{:S(2)}) copy-start(f32[2048,128]{1,0:T(8,128)} %get-tuple-element.17) | copy-start | bytes 3145732

commit v3 on v2

v3 whole, which is shorter than its diff:
```python
import functools

import jax
import jax.numpy as jnp
from jax import lax
from jax.experimental import pallas as pl
from jax.experimental.pallas import tpu as pltpu
from jax.sharding import PartitionSpec as P

SWEEPS = 4
STEP_WEIGHT = 0.5
CHUNK = 1024
SLOTS = 4
GROUPS = ((0, 64), (64, 64))
SHIPPED = 640
ROW_BLOCKS = 4
KEPT = 4
PIECES = (6, 5, 1)
MESH = pl.DeviceIdType.MESH


def dot_t(left, right):
    return lax.dot_general(left, right, (((1,), (1,)), ((), ())), preferred_element_type=jnp.float32)


def sweep_kernel(
    total_rows, x_hbm, y_hbm, w0_hbm, eta_hbm, lam_hbm,
    r_hbm, shipped_hbm, w_near, w_far, *rest,
):
    w_pieces, rest = rest[: len(PIECES)], rest[len(PIECES):]
    (
        xbuf, w0buf, gsend, grecv, sbuf, wt, ut, acc, rt, rbt, ra, uall, eta_ref, lam_ref, lam_col,
        x_sem, w0_sem, in_sem, ship_sem, r_send, r_recv, g_send, g_recv, s_send, s_recv, f_send, f_recv, u_send, u_recv, w_send, w_recv, out_sem,
    ) = rest
    z, s, f = lax.axis_index("problem"), lax.axis_index("samp"), lax.axis_index("feat")
    chunks, targets, _ = wt.shape
    core, chip = f % 2, f // 2
    near = chip * 2 + (1 - core)
    far = (1 - chip) * 2 + core
    partner_id = (z, 1 - s, f)
    near_id, far_id = (z, s, near), (z, s, far)
    own, other = s, 1 - s

    barrier = pltpu.get_barrier_semaphore()
    for device in (partner_id, near_id, far_id):
        pl.semaphore_signal(barrier, inc=1, device_id=device, device_id_type=MESH)

    def columns_of(chunk):
        return pl.ds(pl.multiple_of(chunk * CHUNK, CHUNK), CHUNK)

    def x_load(chunk, slot):
        return pltpu.make_async_copy(x_hbm.at[:, columns_of(chunk)], xbuf.at[slot], x_sem.at[slot, 0])

    def w0_load(chunk, slot):
        return pltpu.make_async_copy(w0_hbm.at[columns_of(chunk), :], w0buf.at[slot], w0_sem.at[slot])

    def part(ref, g, k):
        return ref.at[k, pl.ds(*GROUPS[g]), :]

    def rows_of(g):
        return pl.ds(*GROUPS[g])

    def g_copy(g, k):
        return pltpu.make_async_remote_copy(
            src_ref=part(gsend, g, k), dst_ref=part(grecv, g, k), send_sem=g_send.at[g, k], recv_sem=g_recv.at[g, k],
            device_id=partner_id, device_id_type=MESH)

    def s_copy(g, k):
        return pltpu.make_async_remote_copy(
            src_ref=part(sbuf, g, k), dst_ref=part(sbuf, g, chunks + k), send_sem=s_send.at[g, k], recv_sem=s_recv.at[g, k],
            device_id=partner_id, device_id_type=MESH)

    def u_copy(parity, g, slot, which, device):
        rows = uall.at[parity, slot, rows_of(g), :]
        return pltpu.make_async_remote_copy(
            src_ref=rows, dst_ref=rows,
            send_sem=u_send.at[parity, g, which], recv_sem=u_recv.at[parity, g, which],
            device_id=device, device_id_type=MESH)

    ahead = SLOTS - 1

    def start(copy):
        copy.start(priority=1)

    def wait(copy):
        copy.wait()

    def other_load(i, slot, act):
        act(x_load(other * chunks + i, slot))

    def own_load(i, slot, act):
        @pl.when(i != chunks - 1)
        def _():
            act(x_load(own * chunks + i - i // chunks, slot))

        @pl.when(i == chunks - 1)
        def _():
            act(pltpu.make_async_copy(shipped_hbm, xbuf.at[slot, :, pl.ds(0, SHIPPED)], x_sem.at[slot, 0]))

    def steps(base, count, load, next_load, body, more=None):
        def step(i, carry):
            upcoming = i + ahead
            slot = (base + upcoming) % SLOTS

            @pl.when(upcoming < count)
            def _():
                load(upcoming, slot, start)

            wanted = upcoming >= count
            if more is not None:
                wanted = jnp.logical_and(wanted, more)

            @pl.when(wanted)
            def _():
                next_load(upcoming - count, slot, start)

            load(i, (base + i) % SLOTS, wait)
            body(i, (base + i) % SLOTS)
            return carry

        lax.fori_loop(0, count, step, 0)

    rows = x_hbm.shape[0] // ROW_BLOCKS
    width = xbuf.shape[1] // rows
    passes = 2 * chunks // width
    blocks = ROW_BLOCKS * passes
    pairs = w0buf.shape[0] // 2

    def tile_load(step, q):
        slot = step % SLOTS
        where = pl.ds(pl.multiple_of(step // passes * rows, rows), rows)
        return pltpu.make_async_copy(
            x_hbm.at[where, columns_of(step % passes * width + q)], xbuf.at[slot, pl.ds(q * rows, rows), :], x_sem.at[slot, q])

    def tiles_ahead(step):
        upcoming = step + ahead

        @pl.when(upcoming < blocks)
        def _():
            for q in range(width):
                tile_load(upcoming, q).start(priority=1)

        @pl.when(upcoming >= blocks)
        def _():
            x_load(other * chunks + upcoming - blocks, upcoming % SLOTS).start(priority=1)

    def w0_pair(pair, q):
        return w0_load(2 * pair + q, 2 * (pair % pairs) + q)

    eta_load = pltpu.make_async_copy(eta_hbm, eta_ref, in_sem.at[0])
    lam_load = pltpu.make_async_copy(lam_hbm, lam_ref, in_sem.at[1])
    halves = [
        pltpu.make_async_copy(
            y_hbm.at[pl.ds(i * CHUNK, CHUNK), :], w0buf.at[2 * pairs - 2 + i], w0_sem.at[2 * pairs - 2 + i])
        for i in range(2)
    ]
    for load in (*halves, lam_load, eta_load):
        load.start()
    for pair in range(pairs - 1):
        for q in range(2):
            w0_pair(pair, q).start()
    for step in range(ahead):
        for q in range(width):
            tile_load(step, q).start(priority=1)
    ut[...] = jnp.zeros_like(ut)
    acc[...] = jnp.zeros_like(acc)
    for i, load in enumerate(halves):
        load.wait()
        rt[:, i * CHUNK:(i + 1) * CHUNK] = w0buf[2 * pairs - 2 + i].T
    pl.semaphore_wait(barrier, 3)
    ship = pltpu.make_async_remote_copy(
        src_ref=x_hbm.at[:, pl.ds(pl.multiple_of((other + 1) * chunks * CHUNK - SHIPPED, 128), SHIPPED)],
        dst_ref=shipped_hbm, send_sem=ship_sem.at[0], recv_sem=ship_sem.at[1],
        device_id=partner_id, device_id_type=MESH)
    ship.start()
    lam_load.wait()
    lam_col[...] = jnp.broadcast_to(lam_ref[0:1, :], (targets, targets)).T

    def first_pass(pair, carry):
        @pl.when(pair % (width // 2) == 0)
        def _():
            tiles_ahead(pair // (width // 2))

        @pl.when(pair + pairs - 1 < chunks)
        def _():
            for q in range(2):
                w0_pair(pair + pairs - 1, q).start()

        slot = pair // (width // 2) % SLOTS
        first = pair % (width // 2) * 2
        total = acc[...]
        for q in range(2):
            w0_pair(pair, q).wait()
            tile_load(pair // (width // 2), first + q).wait()
        for q in range(2):
            turned = w0buf[2 * (pair % pairs) + q].T.astype(jnp.bfloat16)
            sbuf[2 * pair + q] = turned
            where = pl.ds(pl.multiple_of((first + q) * rows, rows), rows)
            total += dot_t(turned, xbuf[slot, where, :])
        acc[...] = total
        return carry

    def later_pass(block, carry):
        def step_(i, inner):
            step = block * passes + i
            tiles_ahead(step)
            for q in range(width):
                tile_load(step, q).wait()
            slot = step % SLOTS
            total = acc[...]
            for q in range(width):
                total += dot_t(sbuf[i * width + q], xbuf[slot, q * rows:(q + 1) * rows, :])
            acc[...] = total
            return inner

        lax.fori_loop(0, passes, step_, 0)
        return carry

    def lanes_of(block):
        return pl.ds(block * rows, rows)

    def first_copy(block, g, slot, which, device):
        ref = uall.at[0, slot, rows_of(g), lanes_of(block)]
        return pltpu.make_async_remote_copy(
            src_ref=ref, dst_ref=ref, send_sem=f_send.at[block, g, which], recv_sem=f_recv.at[block, g, which],
            device_id=device, device_id_type=MESH)

    def first_begin(block):
        uall[0, f, :, lanes_of(block)] = acc[...].astype(jnp.bfloat16)
        acc[...] = jnp.zeros_like(acc)
        for g in range(len(GROUPS)):
            first_copy(block, g, f, 0, near_id).start()
            first_copy(block, g, f, 1, far_id).start()

    def first_forward(block, g):
        first_copy(block, g, far, 1, far_id).wait_recv()
        first_copy(block, g, far, 2, near_id).start()

    def first_end(block, g):
        first_copy(block, g, near, 0, near_id).wait_recv()
        first_copy(block, g, far, 2, near_id).wait_recv()
        total = uall[0, 0, rows_of(g), lanes_of(block)].astype(jnp.float32)
        for j in range(1, 4):
            total += uall[0, j, rows_of(g), lanes_of(block)].astype(jnp.float32)
        new = rt[rows_of(g), lanes_of(block)] - total
        rt[rows_of(g), lanes_of(block)] = new
        rbt[rows_of(g), lanes_of(block)] = new.astype(jnp.bfloat16)
        first_copy(block, g, f, 0, near_id).wait_send()
        first_copy(block, g, f, 1, far_id).wait_send()
        first_copy(block, g, far, 2, near_id).wait_send()

    lax.fori_loop(0, chunks, first_pass, 0)
    last = ROW_BLOCKS - 1
    for block in range(ROW_BLOCKS):
        if block:
            later_pass(block, 0)
        first_begin(block)
        for g in range(len(GROUPS)):
            if block >= 1:
                first_forward(block - 1, g)
            if block >= 2:
                first_end(block - 2, g)

    def u_begin(parity, g):
        uall[parity, f, rows_of(g), :] = ut[rows_of(g), :].astype(jnp.bfloat16)
        ut[rows_of(g), :] = jnp.zeros((GROUPS[g][1], ut.shape[1]), jnp.float32)
        u_copy(parity, g, f, 0, near_id).start()
        u_copy(parity, g, f, 1, far_id).start()

    def u_end(parity, g):
        u_copy(parity, g, far, 1, far_id).wait_recv()
        u_copy(parity, g, far, 2, near_id).start()
        u_copy(parity, g, near, 0, near_id).wait_recv()
        u_copy(parity, g, far, 2, near_id).wait_recv()
        total = uall[parity, 0, rows_of(g), :].astype(jnp.float32)
        for block in range(1, 4):
            total += uall[parity, block, rows_of(g), :].astype(jnp.float32)
        new = rt[rows_of(g), :] - STEP_WEIGHT * total
        rt[rows_of(g), :] = new
        rbt[rows_of(g), :] = new.astype(jnp.bfloat16)
        u_copy(parity, g, f, 0, near_id).wait_send()
        u_copy(parity, g, f, 1, far_id).wait_send()
        u_copy(parity, g, far, 2, near_id).wait_send()

    quarter = ra.shape[1] // 4

    def r_copy(g, source, of, which, device):
        lanes = pl.ds(pl.multiple_of(of * quarter, quarter), quarter)
        return pltpu.make_async_remote_copy(
            src_ref=source.at[rows_of(g), lanes], dst_ref=ra.at[rows_of(g), lanes],
            send_sem=r_send.at[g, which], recv_sem=r_recv.at[g, which], device_id=device, device_id_type=MESH)

    def r_begin(g):
        r_copy(g, rbt, f, 0, partner_id).start()

    def r_spread(g):
        r_copy(g, rbt, f, 0, partner_id).wait()
        r_copy(g, ra, f, 1, near_id).start()
        r_copy(g, ra, f, 2, far_id).start()

    def r_end(g):
        r_copy(g, ra, far, 2, far_id).wait_recv()
        r_copy(g, ra, far, 3, near_id).start()
        r_copy(g, ra, near, 1, near_id).wait_recv()
        r_copy(g, ra, far, 3, near_id).wait_recv()
        r_copy(g, ra, f, 1, near_id).wait_send()
        r_copy(g, ra, f, 2, far_id).wait_send()
        r_copy(g, ra, far, 3, near_id).wait_send()

    sent = CHUNK - SHIPPED

    def last_copy(g):
        lanes = pl.ds(0, sent)
        return pltpu.make_async_remote_copy(
            src_ref=gsend.at[chunks - 1, rows_of(g), lanes], dst_ref=grecv.at[chunks - 1, rows_of(g), lanes],
            send_sem=g_send.at[g, chunks - 1], recv_sem=g_recv.at[g, chunks - 1],
            device_id=partner_id, device_id_type=MESH)

    def for_g_copy(g, k, act):
        @pl.when(k < chunks - 1)
        def _():
            act(g_copy(g, k))

        @pl.when(k == chunks - 1)
        def _():
            act(last_copy(g))

    def partner_gradient(g, base, next_load):
        def body(k, slot):
            @pl.when(k > 0)
            def _():
                g_copy(g, k - 1).start()

            gsend[k, rows_of(g), :] = jnp.dot(rbt[rows_of(g), :], xbuf[slot], preferred_element_type=jnp.float32)

        steps(base, chunks, other_load, next_load, body)
        last_copy(g).start()

    def own_columns(g, t, base, next_load):
        lam = lam_col[rows_of(g), 0:1]

        def body(i, slot):
            @pl.when(i == chunks - 1)
            def _():
                r_end(g)
                grecv[chunks - 1, rows_of(g), sent:] = jnp.dot(
                    ra[rows_of(g), :], xbuf[slot, :, 0:SHIPPED], preferred_element_type=jnp.float32)

            @pl.when(i != chunks - 1)
            def _():
                k = i - i // chunks
                for_g_copy(g, k, lambda copy: copy.wait_recv())

                @pl.when(t > 0)
                def _():
                    s_copy(g, k).wait_send()

                mine = jnp.dot(rbt[rows_of(g), :], xbuf[slot], preferred_element_type=jnp.float32)
                weights = wt[k, rows_of(g), :]
                gradient = (mine + grecv[k, rows_of(g), :]) * (1.0 / total_rows)
                lanes = eta_ref.shape[1]
                first = (own * chunks + k) * (CHUNK // lanes)
                eta = jnp.concatenate([eta_ref[pl.ds(first + j, 1), :] for j in range(CHUNK // lanes)], axis=1)
                delta = eta * (gradient - lam * weights)
                wt[k, rows_of(g), :] = weights + STEP_WEIGHT * delta
                delta_b = delta.astype(jnp.bfloat16)
                sbuf[k, rows_of(g), :] = delta_b
                ut[rows_of(g), :] += dot_t(delta_b, xbuf[slot])
                s_copy(g, k).start()

        steps(base, chunks + 1, own_load, next_load, body)

    def partner_columns(g, base, next_load, more=None):
        def body(k, slot):
            s_copy(g, k).wait_recv()
            for_g_copy(g, k, lambda copy: copy.wait_send())
            ut[rows_of(g), :] += dot_t(sbuf[chunks + k, rows_of(g), :], xbuf[slot])

        steps(base, chunks, other_load, next_load, body, more)

    first_forward(last, 0)
    first_end(last - 1, 0)
    first_end(last, 0)
    r_begin(0)
    first_forward(last, 1)
    partner_gradient(0, blocks, other_load)
    first_end(last - 1, 1)
    first_end(last, 1)
    r_begin(1)
    partner_gradient(1, blocks, own_load)

    eta_load.wait()
    for k in range(ahead):
        w0_load(own * chunks + k, k).start()

    def keep(k, carry):
        @pl.when(k + ahead < chunks)
        def _():
            w0_load(own * chunks + k + ahead, (k + ahead) % SLOTS).start()

        w0_load(own * chunks + k, k % SLOTS).wait()
        wt[k] = w0buf[k % SLOTS].T
        return carry

    lax.fori_loop(0, chunks, keep, 0)
    ship.wait()
    r_spread(0)

    def w_store(ref, first, n, k):
        rows = pl.ds(pl.multiple_of(k * CHUNK, CHUNK), CHUNK)
        slot = (first + k) % SLOTS
        return pltpu.make_async_copy(w0buf.at[slot], ref.at[rows, :], out_sem.at[slot])

    def w_copy(k):
        rows = pl.ds(pl.multiple_of(k * CHUNK, CHUNK), CHUNK)
        slot = k % SLOTS
        return pltpu.make_async_remote_copy(
            src_ref=w0buf.at[slot], dst_ref=w_far.at[rows, :], send_sem=w_send.at[slot], recv_sem=w_recv.at[slot],
            device_id=partner_id, device_id_type=MESH)

    def w_out():
        first = 0
        for ref, n in (*zip(w_pieces, PIECES), (w_near, KEPT)):

            def put(k, carry, ref=ref, n=n, first=first):
                chunk = first + k
                slot = chunk % SLOTS

                @pl.when(chunk >= SLOTS)
                def _():
                    w_store(ref, first, n, k).wait()

                w0buf[slot] = wt[chunk].T
                w_store(ref, first, n, k).start()
                return carry

            lax.fori_loop(0, n, put, 0)
            first += n

        def send(k, carry):
            w_copy(k).start()
            return carry

        lax.fori_loop(0, KEPT, send, 0)

    def sweep(t, carry):
        parity = (t + 1) % 2
        more = t < SWEEPS - 1
        at = t * (6 * chunks + 2)
        own_columns(0, t, at, own_load)
        r_spread(1)
        own_columns(1, t, at + chunks + 1, other_load)

        @pl.when(jnp.logical_not(more))
        def _():
            w_out()

        at = at + 2 * chunks + 2
        partner_columns(0, at, other_load)
        u_begin(parity, 0)
        u_end(parity, 0)

        @pl.when(more)
        def _():
            r_begin(0)
            partner_gradient(0, at, other_load)

        partner_columns(1, at, other_load, more)

        @pl.when(more)
        def _():
            r_spread(0)

        u_begin(parity, 1)
        u_end(parity, 1)

        @pl.when(more)
        def _():
            r_begin(1)
            partner_gradient(1, at, own_load)

        return carry

    lax.fori_loop(0, SWEEPS, sweep, 0)
    r_stores = []
    for i in range(2):
        w0buf[SLOTS + i] = rt[:, i * CHUNK:(i + 1) * CHUNK].T
        r_stores.append(
            pltpu.make_async_copy(w0buf.at[SLOTS + i], r_hbm.at[pl.ds(i * CHUNK, CHUNK), :], in_sem.at[i]))
        r_stores[i].start()

    def drain(k, carry):
        for g in range(len(GROUPS)):
            s_copy(g, k).wait_send()
        return carry

    lax.fori_loop(0, chunks, drain, 0)
    for k in range(KEPT):
        w_store(w_near, sum(PIECES), KEPT, k).wait()
        w_copy(k).wait()
    for store in r_stores:
        store.wait()


def place(result, piece, half, first, shape, extra=None):
    rows, width = piece.shape
    halves = shape[0] // CHUNK // 2
    here = pl.BlockSpec((CHUNK, width), lambda i, half_ref: (half_ref[0] * halves + first + i, 0))
    out_shape, out_specs = [jax.ShapeDtypeStruct(shape, piece.dtype)], [here]

    def body(half_ref, piece_ref, other_ref, out_ref, *copied):
        out_ref[...] = piece_ref[...]
        for ref in copied:
            ref[...] = other_ref[...]

    if result is None:
        whole = pl.BlockSpec(extra.shape, lambda i, half_ref: (0, 0))
        out_shape.append(jax.ShapeDtypeStruct(extra.shape, extra.dtype))
        out_specs.append(whole)
        other, other_spec, aliases = extra, whole, {}
    else:
        other, other_spec, aliases = result, pl.BlockSpec(memory_space=pl.ANY), {2: 0}
    return pl.pallas_call(
        body,
        name="place",
        out_shape=out_shape,
        grid_spec=pltpu.PrefetchScalarGridSpec(
            num_scalar_prefetch=1,
            grid=(rows // CHUNK,),
            in_specs=[pl.BlockSpec((CHUNK, width), lambda i, half_ref: (i, 0)), other_spec],
            out_specs=out_specs,
        ),
        input_output_aliases=aliases,
    )(half, piece, other)


def solution(mesh):
    samp_size = mesh.shape["samp"]
    design_spec = P(("problem", "samp"), "feat")
    rows_spec = P(("problem", "samp"), None)
    coef_spec = P(("problem", "feat"), None)
    step_spec = P(("problem", "feat"))
    ridge_spec = P("problem")

    def local_sweeps(design, targets, coef_init, step_sizes, ridge_weights):
        rows, columns = design.shape
        width = targets.shape[1]
        groups = len(GROUPS)
        chunks = columns // CHUNK // samp_size
        bf16, f32 = jnp.bfloat16, jnp.float32
        vmem, dma = pltpu.VMEM, pltpu.SemaphoreType.DMA
        in_hbm = pl.BlockSpec(memory_space=pltpu.HBM)
        sizes = (KEPT, KEPT, *PIECES)
        resid, _, near, far, *pieces = pl.pallas_call(
            functools.partial(sweep_kernel, rows * samp_size),
            name="sweeps",
            out_shape=(
                jax.ShapeDtypeStruct((rows, width), f32),
                jax.ShapeDtypeStruct((rows, SHIPPED), bf16),
                *(jax.ShapeDtypeStruct((n * CHUNK, width), f32) for n in sizes),
            ),
            in_specs=[in_hbm] * 5,
            out_specs=(in_hbm,) * (2 + len(sizes)),
            scratch_shapes=[
                vmem((SLOTS, rows, CHUNK), bf16),
                vmem((SLOTS + 2, CHUNK, width), f32),
                vmem((chunks, width, CHUNK), f32),
                vmem((chunks, width, CHUNK), f32),
                vmem((2 * chunks, width, CHUNK), bf16),
                vmem((chunks, width, CHUNK), f32),
                vmem((width, rows), f32),
                vmem((width, rows // ROW_BLOCKS), f32),
                vmem((width, rows), f32),
                vmem((width, rows), bf16),
                vmem((width, rows), bf16),
                vmem((2, 4, width, rows), bf16),
                vmem((columns // 128, 128), f32),
                vmem((1, width), f32),
                vmem((width, width), f32),
                dma((SLOTS, ROW_BLOCKS)),
                dma((SLOTS + 2,)),
                dma((2,)),
                dma((2,)),
                dma((groups, 4)),
                dma((groups, 4)),
                dma((groups, chunks)),
                dma((groups, chunks)),
                dma((groups, chunks)),
                dma((groups, chunks)),
                dma((ROW_BLOCKS, groups, 3)),
                dma((ROW_BLOCKS, groups, 3)),
                dma((2, groups, 3)),
                dma((2, groups, 3)),
                dma((SLOTS,)),
                dma((SLOTS,)),
                dma((SLOTS,)),
            ],
            compiler_params=pltpu.CompilerParams(
                collective_id=0, has_side_effects=True, vmem_limit_bytes=67_000_000),
        )(design, targets, coef_init, step_sizes.reshape(columns // 128, 128), ridge_weights.reshape(1, width))
        here = lax.axis_index("samp").astype(jnp.int32).reshape(1)
        swap = [(i, samp_size - 1 - i) for i in range(samp_size)]
        arrived = [lax.ppermute(piece, "samp", swap) for piece in pieces]
        shape = (columns, width)
        coef, resid = place(None, near, here, sum(PIECES), shape, resid)
        for half, parts in ((here, pieces), (1 - here, arrived)):
            first = 0
            for piece, n in zip(parts, PIECES):
                (coef,) = place(coef, piece, half, first, shape)
                if half is here and first == 0:
                    (coef,) = place(coef, far, 1 - here, sum(PIECES), shape)
                first += n
        return coef, resid

    return jax.shard_map(
        local_sweeps, mesh=mesh, in_specs=(design_spec, rows_spec, coef_spec, step_spec, ridge_spec),
        out_specs=(coef_spec, rows_spec), check_vma=False)
```

time: 1340 us -> 1320 us (0.985)
    pallas_call x1, Pallas kernels: 1190 us -> 1170 us  [local_sweeps(): pl.pallas_call(functools.partial(sweep_kernel, rows * samp_size), name='s...]
where the time goes in v3:
time: 1320 us; the launch traced here: 1310 us
  Pallas kernels  1210 us (92%)
  waiting for transfers between devices  103 us (8%)
    pallas_call x1, Pallas kernels, local_sweeps(): pl.pallas_call(functools.partial(sweep_kernel, rows * samp_size), name='s...  1170 us
    ppermute x3, waiting for transfers between devices, local_sweeps(): arrived = [lax.ppermute(piece, 'samp', swap) for piece in pieces]  103 us
    pallas_call x8, Pallas kernels, place(): pl.pallas_call(body, name='place', out_shape=out_shape, grid_spec=pltpu.P...  31.9 us
  transfers between devices with their start and end apart: 3, of which 3 were waited for; matrix products, arithmetic and copies ran while one was open for 0% of the time, Pallas kernels for 2%

profile of v3, /device:TPU:0, one launch (start us, length us, event | category | flops | bytes accessed | tf_op | source)
XLA Modules:
  0.0 1314.4 jit_solution(6804150746882426234)
XLA Ops:
  0.6 1174.5 %sweeps.1 = (f32[2048,128]{1,0:T(8,128)}, bf16[2048,640]{1,0:T(8,128)(2,1)}, f32[4096,128]{1,0:T(8,128)}, f32[4096,128]{1,0:T(8,128)}, f32[6144,128]{1,0:T(8,128...) custom-call(bf16[2048,32768]{1,0:T(8,128)(2,1)} %x_hbm.1, f32[2048,128]{1,0:T(8,128)} %y_hbm.1, f32[32768,128]{1,0:T(8,128)} %w0_hbm.1, ...), custom_call_target="tpu_custom_call" | custom-call | tf_op jit(solution)/shard_map/sweeps/pallas_call | solution.py:554
  1175.1 0.5 collective-permute-start.2
  1175.7 1.5 collective-permute-start.1
  1177.2 0.5 collective-permute-start
  1177.7 4.5 place.8
  1182.2 5.3 place.9.other_ref
  1187.4 3.8 place.10.other_ref
  1191.2 4.7 place.11.other_ref
  1195.9 1.9 place.12.other_ref
  1197.8 48.4 %collective-permute-done.2.piece_ref = f32[6144,128]{1,0:T(8,128)S(1)} collective-permute-done((f32[6144,128]{1,0:T(8,128)}, f32[6144,128]{1,0:T(8,128)S(1)}, u32[]{:S(2)}, u32[]{:S(2)}) %collective-permute-start.2) | collective-permute-done | bytes 3145760 | tf_op jit(solution)/shard_map/ppermute | solution.py:603
  1246.1 0.0 copy-start
  1246.1 1.7 copy-done
  1247.8 5.3 place.13.other_ref
  1253.1 49.3 %collective-permute-done.1.piece_ref = f32[5120,128]{1,0:T(8,128)} collective-permute-done((f32[5120,128]{1,0:T(8,128)}, f32[5120,128]{1,0:T(8,128)}, u32[]{:S(2)}, u32[]{:S(2)}) %collective-permute-start.1) | collective-permute-done | bytes 2621472 | tf_op jit(solution)/shard_map/ppermute | solution.py:603
  1302.3 4.7 place.14.other_ref
  1307.0 5.5 collective-permute-done.piece_ref
  1312.5 1.9 place.15
Async XLA Ops:
  1175.1 71.0 %collective-permute-start.2 = (f32[6144,128]{1,0:T(8,128)}, f32[6144,128]{1,0:T(8,128)S(1)}, u32[]{:S(2)}, u32[]{:S(2)}) collective-permute-start(f32[6144,128]{1,0:T(8,128)} %get-tuple-element.12.piece_ref), channel_id=1, source_target_pairs={{0,4},{4,0},{1,5},{5,1},{2,6},{6,2},{3,7},{7,3}} | collective-permute-start | bytes 9437192 | tf_op jit(solution)/shard_map/ppermute | solution.py:603
  1175.7 126.6 %collective-permute-start.1 = (f32[5120,128]{1,0:T(8,128)}, f32[5120,128]{1,0:T(8,128)}, u32[]{:S(2)}, u32[]{:S(2)}) collective-permute-start(f32[5120,128]{1,0:T(8,128)} %get-tuple-element.11.piece_ref), channel_id=1, source_target_pairs={{0,4},{4,0},{1,5},{5,1},{2,6},{6,2},{3,7},{7,3}} | collective-permute-start | bytes 7864328 | tf_op jit(solution)/shard_map/ppermute | solution.py:603
  1177.2 135.3 %collective-permute-start = (f32[1024,128]{1,0:T(8,128)}, f32[1024,128]{1,0:T(8,128)}, u32[]{:S(2)}, u32[]{:S(2)}) collective-permute-start(f32[1024,128]{1,0:T(8,128)} %get-tuple-element.10.piece_ref), channel_id=1, source_target_pairs={{0,4},{4,0},{1,5},{5,1},{2,6},{6,2},{3,7},{7,3}} | collective-permute-start | bytes 1572872 | tf_op jit(solution)/shard_map/ppermute | solution.py:603
  1246.1 1.7 copy-start

commit v4 on v3

--- a/solution.py
+++ b/solution.py
@@ -12,7 +12,7 @@
 CHUNK = 1024
 SLOTS = 4
 GROUPS = ((0, 64), (64, 64))
-SHIPPED = 640
+SHIPPED = 512
 ROW_BLOCKS = 4
 KEPT = 4
 PIECES = (6, 5, 1)
@@ -29,7 +29,7 @@
 ):
     w_pieces, rest = rest[: len(PIECES)], rest[len(PIECES):]
     (
-        xbuf, w0buf, gsend, grecv, sbuf, wt, ut, acc, rt, rbt, ra, uall, eta_ref, lam_ref, lam_col,
+        xbuf, turned, w0buf, gsend, grecv, sbuf, wt, ut, acc, rt, rbt, ra, uall, eta_ref, lam_ref, lam_col,
         x_sem, w0_sem, in_sem, ship_sem, r_send, r_recv, g_send, g_recv, s_send, s_recv, f_send, f_recv, u_send, u_recv, w_send, w_recv, out_sem,
     ) = rest
     z, s, f = lax.axis_index("problem"), lax.axis_index("samp"), lax.axis_index("feat")
@@ -193,12 +193,21 @@
             w0_pair(pair, q).wait()
             tile_load(pair // (width // 2), first + q).wait()
         for q in range(2):
-            turned = w0buf[2 * (pair % pairs) + q].T.astype(jnp.bfloat16)
-            sbuf[2 * pair + q] = turned
+            weights = w0buf[2 * (pair % pairs) + q].T.astype(jnp.bfloat16)
+            sbuf[2 * pair + q] = weights
             where = pl.ds(pl.multiple_of((first + q) * rows, rows), rows)
-            total += dot_t(turned, xbuf[slot, where, :])
+            total += dot_t(weights, xbuf[slot, where, :])
         acc[...] = total
         return carry
+
+    def block_product(weights, tiles):
+        plain = len(tiles) // 2
+        for q, tile in enumerate(tiles[plain:]):
+            turned[q] = tile.T
+        total = sum(dot_t(weight, tile) for weight, tile in zip(weights[:plain], tiles))
+        for q, weight in enumerate(weights[plain:]):
+            total += jnp.dot(weight, turned[q], preferred_element_type=jnp.float32)
+        return total
 
     def later_pass(block, carry):
         def step_(i, inner):
@@ -207,10 +216,9 @@
             for q in range(width):
                 tile_load(step, q).wait()
             slot = step % SLOTS
-            total = acc[...]
-            for q in range(width):
-                total += dot_t(sbuf[i * width + q], xbuf[slot, q * rows:(q + 1) * rows, :])
-            acc[...] = total
+            acc[...] += block_product(
+                [sbuf[i * width + q] for q in range(width)],
+                [xbuf[slot, q * rows:(q + 1) * rows, :] for q in range(width)])
             return inner
 
         lax.fori_loop(0, passes, step_, 0)
@@ -327,14 +335,10 @@
 
     def partner_gradient(g, base, next_load):
         def body(k, slot):
-            @pl.when(k > 0)
-            def _():
-                g_copy(g, k - 1).start()
-
             gsend[k, rows_of(g), :] = jnp.dot(rbt[rows_of(g), :], xbuf[slot], preferred_element_type=jnp.float32)
+            for_g_copy(g, k, lambda copy: copy.start())
 
         steps(base, chunks, other_load, next_load, body)
-        last_copy(g).start()
 
     def own_columns(g, t, base, next_load):
         lam = lam_col[rows_of(g), 0:1]
@@ -563,6 +567,7 @@
             out_specs=(in_hbm,) * (2 + len(sizes)),
             scratch_shapes=[
                 vmem((SLOTS, rows, CHUNK), bf16),
+                vmem((2, CHUNK, rows // ROW_BLOCKS), bf16),
                 vmem((SLOTS + 2, CHUNK, width), f32),
                 vmem((chunks, width, CHUNK), f32),
                 vmem((chunks, width, CHUNK), f32),

time: 1320 us -> 1310 us (level)
  no operation moved by 1% of the time
where the time goes in v4:
time: 1310 us
  Pallas kernels  1200 us (92%)
  waiting for transfers between devices  103 us (8%)
    pallas_call x1, Pallas kernels, local_sweeps(): pl.pallas_call(functools.partial(sweep_kernel, rows * samp_size), name='s...  1170 us
    ppermute x3, waiting for transfers between devices, local_sweeps(): arrived = [lax.ppermute(piece, 'samp', swap) for piece in pieces]  103 us
    pallas_call x8, Pallas kernels, place(): pl.pallas_call(body, name='place', out_shape=out_shape, grid_spec=pltpu.P...  31.9 us
  transfers between devices with their start and end apart: 3, of which 3 were waited for; matrix products, arithmetic and copies ran while one was open for 0% of the time, Pallas kernels for 2%

profile of v4, /device:TPU:0, one launch (start us, length us, event | category | flops | bytes accessed | tf_op | source)
XLA Modules:
  0.0 1310.7 jit_solution(14952564303310043661)
XLA Ops:
  0.6 1170.9 %sweeps.1 = (f32[2048,128]{1,0:T(8,128)}, bf16[2048,512]{1,0:T(8,128)(2,1)}, f32[4096,128]{1,0:T(8,128)}, f32[4096,128]{1,0:T(8,128)}, f32[6144,128]{1,0:T(8,128...) custom-call(bf16[2048,32768]{1,0:T(8,128)(2,1)} %x_hbm.1, f32[2048,128]{1,0:T(8,128)} %y_hbm.1, f32[32768,128]{1,0:T(8,128)} %w0_hbm.1, ...), custom_call_target="tpu_custom_call" | custom-call | tf_op jit(solution)/shard_map/sweeps/pallas_call | solution.py:558
  1171.5 0.5 collective-permute-start.2
  1172.0 1.5 collective-permute-start.1
  1173.6 0.5 collective-permute-start
  1174.1 4.5 place.8
  1178.5 5.3 place.9.other_ref
  1183.8 3.8 place.10.other_ref
  1187.6 4.7 place.11.other_ref
  1192.3 1.9 place.12.other_ref
  1194.1 48.4 %collective-permute-done.2.piece_ref = f32[6144,128]{1,0:T(8,128)S(1)} collective-permute-done((f32[6144,128]{1,0:T(8,128)}, f32[6144,128]{1,0:T(8,128)S(1)}, u32[]{:S(2)}, u32[]{:S(2)}) %collective-permute-start.2) | collective-permute-done | bytes 3145760 | tf_op jit(solution)/shard_map/ppermute | solution.py:608
  1242.5 0.0 copy-start
  1242.5 1.7 copy-done
  1244.2 5.3 place.13.other_ref
  1249.4 49.3 %collective-permute-done.1.piece_ref = f32[5120,128]{1,0:T(8,128)} collective-permute-done((f32[5120,128]{1,0:T(8,128)}, f32[5120,128]{1,0:T(8,128)}, u32[]{:S(2)}, u32[]{:S(2)}) %collective-permute-start.1) | collective-permute-done | bytes 2621472 | tf_op jit(solution)/shard_map/ppermute | solution.py:608
  1298.7 4.7 place.14.other_ref
  1303.4 5.5 collective-permute-done.piece_ref
  1308.9 1.9 place.15
Async XLA Ops:
  1171.5 71.0 %collective-permute-start.2 = (f32[6144,128]{1,0:T(8,128)}, f32[6144,128]{1,0:T(8,128)S(1)}, u32[]{:S(2)}, u32[]{:S(2)}) collective-permute-start(f32[6144,128]{1,0:T(8,128)} %get-tuple-element.12.piece_ref), channel_id=1, source_target_pairs={{0,4},{4,0},{1,5},{5,1},{2,6},{6,2},{3,7},{7,3}} | collective-permute-start | bytes 9437192 | tf_op jit(solution)/shard_map/ppermute | solution.py:608
  1172.0 126.7 %collective-permute-start.1 = (f32[5120,128]{1,0:T(8,128)}, f32[5120,128]{1,0:T(8,128)}, u32[]{:S(2)}, u32[]{:S(2)}) collective-permute-start(f32[5120,128]{1,0:T(8,128)} %get-tuple-element.11.piece_ref), channel_id=1, source_target_pairs={{0,4},{4,0},{1,5},{5,1},{2,6},{6,2},{3,7},{7,3}} | collective-permute-start | bytes 7864328 | tf_op jit(solution)/shard_map/ppermute | solution.py:608
  1173.6 135.3 %collective-permute-start = (f32[1024,128]{1,0:T(8,128)}, f32[1024,128]{1,0:T(8,128)}, u32[]{:S(2)}, u32[]{:S(2)}) collective-permute-start(f32[1024,128]{1,0:T(8,128)} %get-tuple-element.10.piece_ref), channel_id=1, source_target_pairs={{0,4},{4,0},{1,5},{5,1},{2,6},{6,2},{3,7},{7,3}} | collective-permute-start | bytes 1572872 | tf_op jit(solution)/shard_map/ppermute | solution.py:608
  1242.5 1.7 copy-start

commit v5 on v4

--- a/solution.py
+++ b/solution.py
@@ -11,8 +11,9 @@
 STEP_WEIGHT = 0.5
 CHUNK = 1024
 SLOTS = 4
-GROUPS = ((0, 64), (64, 64))
+GROUPS = ((0, 48), (48, 80))
 SHIPPED = 512
+EXTRA = 128
 ROW_BLOCKS = 4
 KEPT = 4
 PIECES = (6, 5, 1)
@@ -88,6 +89,15 @@
     def other_load(i, slot, act):
         act(x_load(other * chunks + i, slot))
 
+    def for_ship(act):
+        @pl.when(core == 0)
+        def _():
+            act(pl.ds(0, EXTRA + SHIPPED))
+
+        @pl.when(core == 1)
+        def _():
+            act(pl.ds(EXTRA, SHIPPED))
+
     def own_load(i, slot, act):
         @pl.when(i != chunks - 1)
         def _():
@@ -95,7 +105,9 @@
 
         @pl.when(i == chunks - 1)
         def _():
-            act(pltpu.make_async_copy(shipped_hbm, xbuf.at[slot, :, pl.ds(0, SHIPPED)], x_sem.at[slot, 0]))
+            for_ship(
+                lambda where: act(
+                    pltpu.make_async_copy(shipped_hbm.at[:, where], xbuf.at[slot, :, where], x_sem.at[slot, 0])))
 
     def steps(base, count, load, next_load, body, more=None):
         def step(i, carry):
@@ -168,11 +180,14 @@
         load.wait()
         rt[:, i * CHUNK:(i + 1) * CHUNK] = w0buf[2 * pairs - 2 + i].T
     pl.semaphore_wait(barrier, 3)
-    ship = pltpu.make_async_remote_copy(
-        src_ref=x_hbm.at[:, pl.ds(pl.multiple_of((other + 1) * chunks * CHUNK - SHIPPED, 128), SHIPPED)],
-        dst_ref=shipped_hbm, send_sem=ship_sem.at[0], recv_sem=ship_sem.at[1],
-        device_id=partner_id, device_id_type=MESH)
-    ship.start()
+
+    def ship(where):
+        first = (other + 1) * chunks * CHUNK - EXTRA - SHIPPED + where.start
+        return pltpu.make_async_remote_copy(
+            src_ref=x_hbm.at[:, pl.ds(pl.multiple_of(first, 128), where.size)], dst_ref=shipped_hbm.at[:, where],
+            send_sem=ship_sem.at[0], recv_sem=ship_sem.at[1], device_id=partner_id, device_id_type=MESH)
+
+    for_ship(lambda where: ship(where).start())
     lam_load.wait()
     lam_col[...] = jnp.broadcast_to(lam_ref[0:1, :], (targets, targets)).T
 
@@ -317,8 +332,8 @@
 
     sent = CHUNK - SHIPPED
 
-    def last_copy(g):
-        lanes = pl.ds(0, sent)
+    def last_copy(g, size):
+        lanes = pl.ds(0, size)
         return pltpu.make_async_remote_copy(
             src_ref=gsend.at[chunks - 1, rows_of(g), lanes], dst_ref=grecv.at[chunks - 1, rows_of(g), lanes],
             send_sem=g_send.at[g, chunks - 1], recv_sem=g_recv.at[g, chunks - 1],
@@ -329,9 +344,11 @@
         def _():
             act(g_copy(g, k))
 
-        @pl.when(k == chunks - 1)
-        def _():
-            act(last_copy(g))
+        for which, size in enumerate((sent - EXTRA, sent)):
+
+            @pl.when(jnp.logical_and(k == chunks - 1, core == which))
+            def _(size=size):
+                act(last_copy(g, size))
 
     def partner_gradient(g, base, next_load):
         def body(k, slot):
@@ -348,7 +365,12 @@
             def _():
                 r_end(g)
                 grecv[chunks - 1, rows_of(g), sent:] = jnp.dot(
-                    ra[rows_of(g), :], xbuf[slot, :, 0:SHIPPED], preferred_element_type=jnp.float32)
+                    ra[rows_of(g), :], xbuf[slot, :, EXTRA:EXTRA + SHIPPED], preferred_element_type=jnp.float32)
+
+                @pl.when(core == 0)
+                def _():
+                    grecv[chunks - 1, rows_of(g), sent - EXTRA:sent] = jnp.dot(
+                        ra[rows_of(g), :], xbuf[slot, :, 0:EXTRA], preferred_element_type=jnp.float32)
 
             @pl.when(i != chunks - 1)
             def _():
@@ -407,7 +429,7 @@
         return carry
 
     lax.fori_loop(0, chunks, keep, 0)
-    ship.wait()
+    for_ship(lambda where: ship(where).wait())
     r_spread(0)
 
     def w_store(ref, first, n, k):
@@ -560,7 +582,7 @@
             name="sweeps",
             out_shape=(
                 jax.ShapeDtypeStruct((rows, width), f32),
-                jax.ShapeDtypeStruct((rows, SHIPPED), bf16),
+                jax.ShapeDtypeStruct((rows, EXTRA + SHIPPED), bf16),
                 *(jax.ShapeDtypeStruct((n * CHUNK, width), f32) for n in sizes),
             ),
             in_specs=[in_hbm] * 5,

time: 1310 us -> 1310 us (level)
  no operation moved by 1% of the time
where the time goes in v5:
time: 1310 us; the launch traced here: 1300 us
  Pallas kernels  1200 us (92%)
  waiting for transfers between devices  103 us (8%)
    pallas_call x1, Pallas kernels, local_sweeps(): pl.pallas_call(functools.partial(sweep_kernel, rows * samp_size), name='s...  1170 us
    ppermute x3, waiting for transfers between devices, local_sweeps(): arrived = [lax.ppermute(piece, 'samp', swap) for piece in pieces]  103 us
    pallas_call x8, Pallas kernels, place(): pl.pallas_call(body, name='place', out_shape=out_shape, grid_spec=pltpu.P...  31.9 us
  transfers between devices with their start and end apart: 3, of which 3 were waited for; matrix products, arithmetic and copies ran while one was open for 0% of the time, Pallas kernels for 2%

profile of v5, /device:TPU:0, one launch (start us, length us, event | category | flops | bytes accessed | tf_op | source)
XLA Modules:
  0.0 1304.9 jit_solution(17986179711051500361)
XLA Ops:
  0.6 1165.4 %sweeps.1 = (f32[2048,128]{1,0:T(8,128)}, bf16[2048,640]{1,0:T(8,128)(2,1)}, f32[4096,128]{1,0:T(8,128)}, f32[4096,128]{1,0:T(8,128)}, f32[6144,128]{1,0:T(8,128...) custom-call(bf16[2048,32768]{1,0:T(8,128)(2,1)} %x_hbm.1, f32[2048,128]{1,0:T(8,128)} %y_hbm.1, f32[32768,128]{1,0:T(8,128)} %w0_hbm.1, ...), custom_call_target="tpu_custom_call" | custom-call | tf_op jit(solution)/shard_map/sweeps/pallas_call | solution.py:580
  1166.1 0.3 collective-permute-start.2
  1166.4 1.7 collective-permute-start.1
  1168.1 0.3 collective-permute-start
  1168.4 4.5 place.8
  1172.9 5.3 place.9.other_ref
  1178.1 3.8 place.10.other_ref
  1181.9 4.7 place.11.other_ref
  1186.6 1.9 place.12.other_ref
  1188.5 47.1 %collective-permute-done.2.piece_ref = f32[6144,128]{1,0:T(8,128)S(1)} collective-permute-done((f32[6144,128]{1,0:T(8,128)}, f32[6144,128]{1,0:T(8,128)S(1)}, u32[]{:S(2)}, u32[]{:S(2)}) %collective-permute-start.2) | collective-permute-done | bytes 3145760 | tf_op jit(solution)/shard_map/ppermute | solution.py:630
  1235.6 0.0 copy-start
  1235.6 1.7 copy-done
  1237.3 5.3 place.13.other_ref
  1242.5 49.3 %collective-permute-done.1.piece_ref = f32[5120,128]{1,0:T(8,128)} collective-permute-done((f32[5120,128]{1,0:T(8,128)}, f32[5120,128]{1,0:T(8,128)}, u32[]{:S(2)}, u32[]{:S(2)}) %collective-permute-start.1) | collective-permute-done | bytes 2621472 | tf_op jit(solution)/shard_map/ppermute | solution.py:630
  1291.8 4.7 place.14.other_ref
  1296.5 6.6 collective-permute-done.piece_ref
  1303.0 1.9 place.15
Async XLA Ops:
  1166.1 69.5 %collective-permute-start.2 = (f32[6144,128]{1,0:T(8,128)}, f32[6144,128]{1,0:T(8,128)S(1)}, u32[]{:S(2)}, u32[]{:S(2)}) collective-permute-start(f32[6144,128]{1,0:T(8,128)} %get-tuple-element.12.piece_ref), channel_id=1, source_target_pairs={{0,4},{4,0},{1,5},{5,1},{2,6},{6,2},{3,7},{7,3}} | collective-permute-start | bytes 9437192 | tf_op jit(solution)/shard_map/ppermute | solution.py:630
  1166.4 125.4 %collective-permute-start.1 = (f32[5120,128]{1,0:T(8,128)}, f32[5120,128]{1,0:T(8,128)}, u32[]{:S(2)}, u32[]{:S(2)}) collective-permute-start(f32[5120,128]{1,0:T(8,128)} %get-tuple-element.11.piece_ref), channel_id=1, source_target_pairs={{0,4},{4,0},{1,5},{5,1},{2,6},{6,2},{3,7},{7,3}} | collective-permute-start | bytes 7864328 | tf_op jit(solution)/shard_map/ppermute | solution.py:630
  1168.1 134.9 %collective-permute-start = (f32[1024,128]{1,0:T(8,128)}, f32[1024,128]{1,0:T(8,128)}, u32[]{:S(2)}, u32[]{:S(2)}) collective-permute-start(f32[1024,128]{1,0:T(8,128)} %get-tuple-element.10.piece_ref), channel_id=1, source_target_pairs={{0,4},{4,0},{1,5},{5,1},{2,6},{6,2},{3,7},{7,3}} | collective-permute-start | bytes 1572872 | tf_op jit(solution)/shard_map/ppermute | solution.py:630
  1235.6 1.7 copy-start

commit v6 on v5

--- a/solution.py
+++ b/solution.py
@@ -31,7 +31,7 @@
     w_pieces, rest = rest[: len(PIECES)], rest[len(PIECES):]
     (
         xbuf, turned, w0buf, gsend, grecv, sbuf, wt, ut, acc, rt, rbt, ra, uall, eta_ref, lam_ref, lam_col,
-        x_sem, w0_sem, in_sem, ship_sem, r_send, r_recv, g_send, g_recv, s_send, s_recv, f_send, f_recv, u_send, u_recv, w_send, w_recv, out_sem,
+        x_sem, w0_sem, in_sem, ship_sem, r_send, r_recv, g_send, g_recv, s_send, s_recv, f_send, f_recv, u_send, u_recv, w_send, w_recv, out_sem, turn_sem,
     ) = rest
     z, s, f = lax.axis_index("problem"), lax.axis_index("samp"), lax.axis_index("feat")
     chunks, targets, _ = wt.shape
@@ -174,20 +174,20 @@
     for step in range(ahead):
         for q in range(width):
             tile_load(step, q).start(priority=1)
+    pl.semaphore_wait(barrier, 3)
+
+    def ship(where):
+        first = (other + 1) * chunks * CHUNK - EXTRA - SHIPPED + where.start
+        return pltpu.make_async_remote_copy(
+            src_ref=x_hbm.at[:, pl.ds(pl.multiple_of(first, 128), where.size)], dst_ref=shipped_hbm.at[:, where],
+            send_sem=ship_sem.at[0], recv_sem=ship_sem.at[1], device_id=partner_id, device_id_type=MESH)
+
+    for_ship(lambda where: ship(where).start())
     ut[...] = jnp.zeros_like(ut)
     acc[...] = jnp.zeros_like(acc)
     for i, load in enumerate(halves):
         load.wait()
         rt[:, i * CHUNK:(i + 1) * CHUNK] = w0buf[2 * pairs - 2 + i].T
-    pl.semaphore_wait(barrier, 3)
-
-    def ship(where):
-        first = (other + 1) * chunks * CHUNK - EXTRA - SHIPPED + where.start
-        return pltpu.make_async_remote_copy(
-            src_ref=x_hbm.at[:, pl.ds(pl.multiple_of(first, 128), where.size)], dst_ref=shipped_hbm.at[:, where],
-            send_sem=ship_sem.at[0], recv_sem=ship_sem.at[1], device_id=partner_id, device_id_type=MESH)
-
-    for_ship(lambda where: ship(where).start())
     lam_load.wait()
     lam_col[...] = jnp.broadcast_to(lam_ref[0:1, :], (targets, targets)).T
 
@@ -444,6 +444,10 @@
             src_ref=w0buf.at[slot], dst_ref=w_far.at[rows, :], send_sem=w_send.at[slot], recv_sem=w_recv.at[slot],
             device_id=partner_id, device_id_type=MESH)
 
+    def w_send_all():
+        for k in range(KEPT):
+            w_copy(k).start()
+
     def w_out():
         first = 0
         for ref, n in (*zip(w_pieces, PIECES), (w_near, KEPT)):
@@ -463,11 +467,9 @@
             lax.fori_loop(0, n, put, 0)
             first += n
 
-        def send(k, carry):
-            w_copy(k).start()
-            return carry
-
-        lax.fori_loop(0, KEPT, send, 0)
+        @pl.when(core == 0)
+        def _():
+            w_send_all()
 
     def sweep(t, carry):
         parity = (t + 1) % 2
@@ -515,6 +517,21 @@
             pltpu.make_async_copy(w0buf.at[SLOTS + i], r_hbm.at[pl.ds(i * CHUNK, CHUNK), :], in_sem.at[i]))
         r_stores[i].start()
 
+    @pl.when(core == 0)
+    def _():
+        for k in range(KEPT - 1):
+            w_copy(k).wait_send()
+        pl.semaphore_signal(turn_sem, inc=1, device_id=near_id, device_id_type=MESH)
+        w_copy(KEPT - 1).wait_send()
+
+    @pl.when(core == 1)
+    def _():
+        pl.semaphore_wait(turn_sem, 1)
+        w_send_all()
+        for k in range(KEPT):
+            w_copy(k).wait_send()
+
+
     def drain(k, carry):
         for g in range(len(GROUPS)):
             s_copy(g, k).wait_send()
@@ -523,7 +540,7 @@
     lax.fori_loop(0, chunks, drain, 0)
     for k in range(KEPT):
         w_store(w_near, sum(PIECES), KEPT, k).wait()
-        w_copy(k).wait()
+        w_copy(k).wait_recv()
     for store in r_stores:
         store.wait()
 
@@ -621,6 +638,7 @@
                 dma((SLOTS,)),
                 dma((SLOTS,)),
                 dma((SLOTS,)),
+                pltpu.SemaphoreType.REGULAR,
             ],
             compiler_params=pltpu.CompilerParams(
                 collective_id=0, has_side_effects=True, vmem_limit_bytes=67_000_000),

time: 1310 us -> 1300 us (level)
  Pallas kernels: 1200 us -> 1180 us
    pallas_call x1, Pallas kernels: 1170 us -> 1150 us  [local_sweeps(): pl.pallas_call(functools.partial(sweep_kernel, rows * samp_size), name='s...]
where the time goes in v6:
time: 1300 us; the launch traced here: 1290 us
  Pallas kernels  1180 us (91%)
  waiting for transfers between devices  99.2 us (8%)
    pallas_call x1, Pallas kernels, local_sweeps(): pl.pallas_call(functools.partial(sweep_kernel, rows * samp_size), name='s...  1150 us
    ppermute x3, waiting for transfers between devices, local_sweeps(): arrived = [lax.ppermute(piece, 'samp', swap) for piece in pieces]  99.2 us
    pallas_call x8, Pallas kernels, place(): pl.pallas_call(body, name='place', out_shape=out_shape, grid_spec=pltpu.P...  31.9 us
  transfers between devices with their start and end apart: 3, of which 3 were waited for; matrix products, arithmetic and copies ran while one was open for 0% of the time, Pallas kernels for 2%

profile of v6, /device:TPU:0, one launch (start us, length us, event | category | flops | bytes accessed | tf_op | source)
XLA Modules:
  0.0 1286.0 jit_solution(17374728653803622797)
XLA Ops:
  0.6 1150.1 %sweeps.1 = (f32[2048,128]{1,0:T(8,128)}, bf16[2048,640]{1,0:T(8,128)(2,1)}, f32[4096,128]{1,0:T(8,128)}, f32[4096,128]{1,0:T(8,128)}, f32[6144,128]{1,0:T(8,128...) custom-call(bf16[2048,32768]{1,0:T(8,128)(2,1)} %x_hbm.1, f32[2048,128]{1,0:T(8,128)} %y_hbm.1, f32[32768,128]{1,0:T(8,128)} %w0_hbm.1, ...), custom_call_target="tpu_custom_call" | custom-call | tf_op jit(solution)/shard_map/sweeps/pallas_call | solution.py:597
  1150.7 0.5 collective-permute-start.2
  1151.3 1.5 collective-permute-start.1
  1152.8 0.5 collective-permute-start
  1153.3 4.5 place.8
  1157.8 5.3 place.9.other_ref
  1163.0 3.8 place.10.other_ref
  1166.8 4.7 place.11.other_ref
  1171.5 1.9 place.12.other_ref
  1173.4 43.4 %collective-permute-done.2.piece_ref = f32[6144,128]{1,0:T(8,128)S(1)} collective-permute-done((f32[6144,128]{1,0:T(8,128)}, f32[6144,128]{1,0:T(8,128)S(1)}, u32[]{:S(2)}, u32[]{:S(2)}) %collective-permute-start.2) | collective-permute-done | bytes 3145760 | tf_op jit(solution)/shard_map/ppermute | solution.py:648
  1216.7 0.0 copy-start
  1216.7 1.7 copy-done
  1218.4 5.3 place.13.other_ref
  1223.6 49.3 %collective-permute-done.1.piece_ref = f32[5120,128]{1,0:T(8,128)} collective-permute-done((f32[5120,128]{1,0:T(8,128)}, f32[5120,128]{1,0:T(8,128)}, u32[]{:S(2)}, u32[]{:S(2)}) %collective-permute-start.1) | collective-permute-done | bytes 2621472 | tf_op jit(solution)/shard_map/ppermute | solution.py:648
  1272.9 4.7 place.14.other_ref
  1277.6 6.6 collective-permute-done.piece_ref
  1284.1 1.9 place.15
Async XLA Ops:
  1150.7 66.0 %collective-permute-start.2 = (f32[6144,128]{1,0:T(8,128)}, f32[6144,128]{1,0:T(8,128)S(1)}, u32[]{:S(2)}, u32[]{:S(2)}) collective-permute-start(f32[6144,128]{1,0:T(8,128)} %get-tuple-element.12.piece_ref), channel_id=1, source_target_pairs={{0,4},{4,0},{1,5},{5,1},{2,6},{6,2},{3,7},{7,3}} | collective-permute-start | bytes 9437192 | tf_op jit(solution)/shard_map/ppermute | solution.py:648
  1151.3 121.6 %collective-permute-start.1 = (f32[5120,128]{1,0:T(8,128)}, f32[5120,128]{1,0:T(8,128)}, u32[]{:S(2)}, u32[]{:S(2)}) collective-permute-start(f32[5120,128]{1,0:T(8,128)} %get-tuple-element.11.piece_ref), channel_id=1, source_target_pairs={{0,4},{4,0},{1,5},{5,1},{2,6},{6,2},{3,7},{7,3}} | collective-permute-start | bytes 7864328 | tf_op jit(solution)/shard_map/ppermute | solution.py:648
  1152.8 131.3 %collective-permute-start = (f32[1024,128]{1,0:T(8,128)}, f32[1024,128]{1,0:T(8,128)}, u32[]{:S(2)}, u32[]{:S(2)}) collective-permute-start(f32[1024,128]{1,0:T(8,128)} %get-tuple-element.10.piece_ref), channel_id=1, source_target_pairs={{0,4},{4,0},{1,5},{5,1},{2,6},{6,2},{3,7},{7,3}} | collective-permute-start | bytes 1572872 | tf_op jit(solution)/shard_map/ppermute | solution.py:648
  1216.7 1.7 copy-start

commit v7 on v6

--- a/solution.py
+++ b/solution.py
@@ -575,6 +575,27 @@
         ),
         input_output_aliases=aliases,
     )(half, piece, other)
+
+
+def place_last(result, piece, half, first):
+    halves = result.shape[0] // CHUNK // 2
+
+    def body(half_ref, piece_ref, result_ref, out_ref, sem):
+        start = pl.multiple_of((half_ref[0] * halves + first) * CHUNK, CHUNK)
+        copy = pltpu.make_async_copy(piece_ref, out_ref.at[pl.ds(start, piece.shape[0]), :], sem)
+        copy.start()
+        copy.wait()
+
+    anywhere = pl.BlockSpec(memory_space=pl.ANY)
+    return pl.pallas_call(
+        body,
+        name="place_last",
+        out_shape=jax.ShapeDtypeStruct(result.shape, result.dtype),
+        grid_spec=pltpu.PrefetchScalarGridSpec(
+            num_scalar_prefetch=1, grid=(1,), in_specs=[pl.BlockSpec(memory_space=pltpu.VMEM), anywhere], out_specs=anywhere,
+            scratch_shapes=[pltpu.SemaphoreType.DMA]),
+        input_output_aliases={2: 0},
+    )(half, pltpu.with_memory_space_constraint(piece, pltpu.VMEM), result)
 
 
 def solution(mesh):
@@ -651,7 +672,10 @@
         for half, parts in ((here, pieces), (1 - here, arrived)):
             first = 0
             for piece, n in zip(parts, PIECES):
-                (coef,) = place(coef, piece, half, first, shape)
+                if half is not here and first + n == sum(PIECES):
+                    coef = place_last(coef, piece, half, first)
+                else:
+                    (coef,) = place(coef, piece, half, first, shape)
                 if half is here and first == 0:
                     (coef,) = place(coef, far, 1 - here, sum(PIECES), shape)
                 first += n

time: 1300 us -> 1300 us (level)
    pallas_call x8 -> x7, Pallas kernels: 31.9 us -> 30 us  [place(): pl.pallas_call(body, name='place', out_shape=out_shape, grid_spec=pltpu.P...]
where the time goes in v7:
time: 1300 us; the launch traced here: 1280 us
  Pallas kernels  1180 us (91%)
  waiting for transfers between devices  101 us (8%)
    pallas_call x1, Pallas kernels, local_sweeps(): pl.pallas_call(functools.partial(sweep_kernel, rows * samp_size), name='s...  1150 us
    ppermute x3, waiting for transfers between devices, local_sweeps(): arrived = [lax.ppermute(piece, 'samp', swap) for piece in pieces]  101 us
    pallas_call x7, Pallas kernels, place(): pl.pallas_call(body, name='place', out_shape=out_shape, grid_spec=pltpu.P...  30 us
  transfers between devices with their start and end apart: 3, of which 3 were waited for; matrix products, arithmetic and copies ran while one was open for 0% of the time, Pallas kernels for 2%

profile of v7, /device:TPU:0, one launch (start us, length us, event | category | flops | bytes accessed | tf_op | source)
XLA Modules:
  0.0 1285.0 jit_solution(15915368425600793133)
XLA Ops:
  0.6 1150.1 %sweeps.1 = (f32[2048,128]{1,0:T(8,128)}, bf16[2048,640]{1,0:T(8,128)(2,1)}, f32[4096,128]{1,0:T(8,128)}, f32[4096,128]{1,0:T(8,128)}, f32[6144,128]{1,0:T(8,128...) custom-call(bf16[2048,32768]{1,0:T(8,128)(2,1)} %x_hbm.1, f32[2048,128]{1,0:T(8,128)} %y_hbm.1, f32[32768,128]{1,0:T(8,128)} %w0_hbm.1, ...), custom_call_target="tpu_custom_call" | custom-call | tf_op jit(solution)/shard_map/sweeps/pallas_call | solution.py:618
  1150.7 0.5 collective-permute-start.2
  1151.3 1.5 collective-permute-start.1
  1152.8 0.5 collective-permute-start
  1153.3 4.5 place.7
  1157.8 5.3 place.8.other_ref
  1163.0 3.8 place.9.other_ref
  1166.8 4.7 place.10.other_ref
  1171.5 1.9 place.11.other_ref
  1173.4 43.2 %collective-permute-done.2.piece_ref = f32[6144,128]{1,0:T(8,128)} collective-permute-done((f32[6144,128]{1,0:T(8,128)}, f32[6144,128]{1,0:T(8,128)}, u32[]{:S(2)}, u32[]{:S(2)}) %collective-permute-start.2) | collective-permute-done | bytes 3145760 | tf_op jit(solution)/shard_map/ppermute | solution.py:669
  1216.6 5.3 place.12.other_ref
  1221.9 50.9 %collective-permute-done.1.piece_ref = f32[5120,128]{1,0:T(8,128)} collective-permute-done((f32[5120,128]{1,0:T(8,128)}, f32[5120,128]{1,0:T(8,128)}, u32[]{:S(2)}, u32[]{:S(2)}) %collective-permute-start.1) | collective-permute-done | bytes 2621472 | tf_op jit(solution)/shard_map/ppermute | solution.py:669
  1272.8 4.7 place.13.result_ref
  1277.5 6.6 collective-permute-done.piece_ref
  1284.0 0.8 place_last.1
Async XLA Ops:
  1150.7 65.9 %collective-permute-start.2 = (f32[6144,128]{1,0:T(8,128)}, f32[6144,128]{1,0:T(8,128)}, u32[]{:S(2)}, u32[]{:S(2)}) collective-permute-start(f32[6144,128]{1,0:T(8,128)} %get-tuple-element.12.piece_ref), channel_id=1, source_target_pairs={{0,4},{4,0},{1,5},{5,1},{2,6},{6,2},{3,7},{7,3}} | collective-permute-start | bytes 9437192 | tf_op jit(solution)/shard_map/ppermute | solution.py:669
  1151.3 121.5 %collective-permute-start.1 = (f32[5120,128]{1,0:T(8,128)}, f32[5120,128]{1,0:T(8,128)}, u32[]{:S(2)}, u32[]{:S(2)}) collective-permute-start(f32[5120,128]{1,0:T(8,128)} %get-tuple-element.11.piece_ref), channel_id=1, source_target_pairs={{0,4},{4,0},{1,5},{5,1},{2,6},{6,2},{3,7},{7,3}} | collective-permute-start | bytes 7864328 | tf_op jit(solution)/shard_map/ppermute | solution.py:669
  1152.8 131.2 %collective-permute-start = (f32[1024,128]{1,0:T(8,128)}, f32[1024,128]{1,0:T(8,128)S(1)}, u32[]{:S(2)}, u32[]{:S(2)}) collective-permute-start(f32[1024,128]{1,0:T(8,128)} %get-tuple-element.10.piece_ref), channel_id=1, source_target_pairs={{0,4},{4,0},{1,5},{5,1},{2,6},{6,2},{3,7},{7,3}} | collective-permute-start | bytes 1572872 | tf_op jit(solution)/shard_map/ppermute | solution.py:669

commit v8 on v7

--- a/solution.py
+++ b/solution.py
@@ -14,7 +14,7 @@
 GROUPS = ((0, 48), (48, 80))
 SHIPPED = 512
 EXTRA = 128
-ROW_BLOCKS = 4
+BLOCKS = ((4, 4), (4, 4), (4, 4), (4, 4))
 KEPT = 4
 PIECES = (6, 5, 1)
 MESH = pl.DeviceIdType.MESH
@@ -31,7 +31,7 @@
     w_pieces, rest = rest[: len(PIECES)], rest[len(PIECES):]
     (
         xbuf, turned, w0buf, gsend, grecv, sbuf, wt, ut, acc, rt, rbt, ra, uall, eta_ref, lam_ref, lam_col,
-        x_sem, w0_sem, in_sem, ship_sem, r_send, r_recv, g_send, g_recv, s_send, s_recv, f_send, f_recv, u_send, u_recv, w_send, w_recv, out_sem, turn_sem,
+        x_sem, w0_sem, in_sem, ship_sem, e_send, e_recv, p_send, p_recv, r_send, r_recv, g_send, g_recv, s_send, s_recv, f_send, f_recv, u_send, u_recv, w_send, w_recv, out_sem, turn_sem,
     ) = rest
     z, s, f = lax.axis_index("problem"), lax.axis_index("samp"), lax.axis_index("feat")
     chunks, targets, _ = wt.shape
@@ -132,29 +132,37 @@
 
         lax.fori_loop(0, count, step, 0)
 
-    rows = x_hbm.shape[0] // ROW_BLOCKS
-    width = xbuf.shape[1] // rows
-    passes = 2 * chunks // width
-    blocks = ROW_BLOCKS * passes
+    sizes = [x_hbm.shape[0] // share for share, _ in BLOCKS]
+    firsts = [sum(sizes[:i]) for i in range(len(sizes))]
+    widths = [width for _, width in BLOCKS]
+    counts = [2 * chunks // width for width in widths]
+    bases = [sum(counts[:i]) for i in range(len(counts))]
+    blocks = sum(counts)
+    rows, width, passes = sizes[0], widths[0], counts[0]
     pairs = w0buf.shape[0] // 2
 
-    def tile_load(step, q):
-        slot = step % SLOTS
-        where = pl.ds(pl.multiple_of(step // passes * rows, rows), rows)
+    def tile_load(block, step, q):
+        slot, size, i = step % SLOTS, sizes[block], step - bases[block]
         return pltpu.make_async_copy(
-            x_hbm.at[where, columns_of(step % passes * width + q)], xbuf.at[slot, pl.ds(q * rows, rows), :], x_sem.at[slot, q])
-
-    def tiles_ahead(step):
+            x_hbm.at[pl.ds(firsts[block], size), columns_of(i * widths[block] + q)],
+            xbuf.at[slot, pl.ds(q * size, size), :], x_sem.at[slot, q])
+
+    def tiles_ahead(block, step):
         upcoming = step + ahead
-
-        @pl.when(upcoming < blocks)
-        def _():
-            for q in range(width):
-                tile_load(upcoming, q).start(priority=1)
-
-        @pl.when(upcoming >= blocks)
-        def _():
-            x_load(other * chunks + upcoming - blocks, upcoming % SLOTS).start(priority=1)
+        reach = bases[block] + counts[block] + ahead
+        for later in range(block, len(BLOCKS)):
+            if bases[later] < reach:
+
+                @pl.when(jnp.logical_and(upcoming >= bases[later], upcoming < bases[later] + counts[later]))
+                def _(later=later):
+                    for q in range(widths[later]):
+                        tile_load(later, upcoming, q).start(priority=1)
+
+        if blocks < reach:
+
+            @pl.when(upcoming >= blocks)
+            def _():
+                x_load(other * chunks + upcoming - blocks, upcoming % SLOTS).start(priority=1)
 
     def w0_pair(pair, q):
         return w0_load(2 * pair + q, 2 * (pair % pairs) + q)
@@ -166,6 +174,14 @@
             y_hbm.at[pl.ds(i * CHUNK, CHUNK), :], w0buf.at[2 * pairs - 2 + i], w0_sem.at[2 * pairs - 2 + i])
         for i in range(2)
     ]
+    end_shipped = (other + 1) * chunks * CHUNK
+
+    def ship(where):
+        first = end_shipped - EXTRA - SHIPPED + where.start
+        return pltpu.make_async_remote_copy(
+            src_ref=x_hbm.at[:, pl.ds(pl.multiple_of(first, 128), where.size)], dst_ref=shipped_hbm.at[:, where],
+            send_sem=ship_sem.at[0], recv_sem=ship_sem.at[1], device_id=partner_id, device_id_type=MESH)
+
     for load in (*halves, lam_load, eta_load):
         load.start()
     for pair in range(pairs - 1):
@@ -173,14 +189,8 @@
             w0_pair(pair, q).start()
     for step in range(ahead):
         for q in range(width):
-            tile_load(step, q).start(priority=1)
+            tile_load(0, step, q).start(priority=1)
     pl.semaphore_wait(barrier, 3)
-
-    def ship(where):
-        first = (other + 1) * chunks * CHUNK - EXTRA - SHIPPED + where.start
-        return pltpu.make_async_remote_copy(
-            src_ref=x_hbm.at[:, pl.ds(pl.multiple_of(first, 128), where.size)], dst_ref=shipped_hbm.at[:, where],
-            send_sem=ship_sem.at[0], recv_sem=ship_sem.at[1], device_id=partner_id, device_id_type=MESH)
 
     for_ship(lambda where: ship(where).start())
     ut[...] = jnp.zeros_like(ut)
@@ -194,7 +204,7 @@
     def first_pass(pair, carry):
         @pl.when(pair % (width // 2) == 0)
         def _():
-            tiles_ahead(pair // (width // 2))
+            tiles_ahead(0, pair // (width // 2))
 
         @pl.when(pair + pairs - 1 < chunks)
         def _():
@@ -206,7 +216,7 @@
         total = acc[...]
         for q in range(2):
             w0_pair(pair, q).wait()
-            tile_load(pair // (width // 2), first + q).wait()
+            tile_load(0, pair // (width // 2), first + q).wait()
         for q in range(2):
             weights = w0buf[2 * (pair % pairs) + q].T.astype(jnp.bfloat16)
             sbuf[2 * pair + q] = weights
@@ -217,30 +227,33 @@
 
     def block_product(weights, tiles):
         plain = len(tiles) // 2
-        for q, tile in enumerate(tiles[plain:]):
-            turned[q] = tile.T
+        size = tiles[0].shape[0]
+        per_slab = turned.shape[2] // size
+        slabs = [turned.at[q // per_slab, :, pl.ds(q % per_slab * size, size)] for q in range(len(tiles) - plain)]
+        for slab, tile in zip(slabs, tiles[plain:]):
+            slab[...] = tile.T
         total = sum(dot_t(weight, tile) for weight, tile in zip(weights[:plain], tiles))
-        for q, weight in enumerate(weights[plain:]):
-            total += jnp.dot(weight, turned[q], preferred_element_type=jnp.float32)
+        for slab, weight in zip(slabs, weights[plain:]):
+            total += jnp.dot(weight, slab[...], preferred_element_type=jnp.float32)
         return total
 
-    def later_pass(block, carry):
+    def later_pass(block):
+        size, some = sizes[block], range(widths[block])
+
         def step_(i, inner):
-            step = block * passes + i
-            tiles_ahead(step)
-            for q in range(width):
-                tile_load(step, q).wait()
+            step = bases[block] + i
+            tiles_ahead(block, step)
+            for q in some:
+                tile_load(block, step, q).wait()
             slot = step % SLOTS
-            acc[...] += block_product(
-                [sbuf[i * width + q] for q in range(width)],
-                [xbuf[slot, q * rows:(q + 1) * rows, :] for q in range(width)])
+            acc[:, 0:size] += block_product(
+                [sbuf[i * widths[block] + q] for q in some], [xbuf[slot, q * size:(q + 1) * size, :] for q in some])
             return inner
 
-        lax.fori_loop(0, passes, step_, 0)
-        return carry
+        lax.fori_loop(0, counts[block], step_, 0)
 
     def lanes_of(block):
-        return pl.ds(block * rows, rows)
+        return pl.ds(firsts[block], sizes[block])
 
     def first_copy(block, g, slot, which, device):
         ref = uall.at[0, slot, rows_of(g), lanes_of(block)]
@@ -249,7 +262,7 @@
             device_id=device, device_id_type=MESH)
 
     def first_begin(block):
-        uall[0, f, :, lanes_of(block)] = acc[...].astype(jnp.bfloat16)
+        uall[0, f, :, lanes_of(block)] = acc[:, 0:sizes[block]].astype(jnp.bfloat16)
         acc[...] = jnp.zeros_like(acc)
         for g in range(len(GROUPS)):
             first_copy(block, g, f, 0, near_id).start()
@@ -272,17 +285,29 @@
         first_copy(block, g, f, 1, far_id).wait_send()
         first_copy(block, g, far, 2, near_id).wait_send()
 
+    piece = rows // 4
+
+    def first_r(block, g=None):
+        rows_g = rows_of(g) if g is not None else pl.ds(0, targets)
+        which = block + (g or 0)
+        lanes = pl.ds(pl.multiple_of(block * rows + f * piece, piece), piece)
+        return pltpu.make_async_remote_copy(
+            src_ref=rbt.at[rows_g, lanes], dst_ref=ra.at[rows_g, lanes],
+            send_sem=e_send.at[which], recv_sem=e_recv.at[which], device_id=partner_id, device_id_type=MESH)
+
     lax.fori_loop(0, chunks, first_pass, 0)
-    last = ROW_BLOCKS - 1
-    for block in range(ROW_BLOCKS):
+    last = len(BLOCKS) - 1
+    for block in range(len(BLOCKS)):
         if block:
-            later_pass(block, 0)
+            later_pass(block)
         first_begin(block)
         for g in range(len(GROUPS)):
             if block >= 1:
                 first_forward(block - 1, g)
             if block >= 2:
                 first_end(block - 2, g)
+        if 2 <= block < 4:
+            first_r(block - 2).start()
 
     def u_begin(parity, g):
         uall[parity, f, rows_of(g), :] = ut[rows_of(g), :].astype(jnp.bfloat16)
@@ -363,7 +388,10 @@
         def body(i, slot):
             @pl.when(i == chunks - 1)
             def _():
-                r_end(g)
+                @pl.when(t > 0)
+                def _():
+                    r_end(g)
+
                 grecv[chunks - 1, rows_of(g), sent:] = jnp.dot(
                     ra[rows_of(g), :], xbuf[slot, :, EXTRA:EXTRA + SHIPPED], preferred_element_type=jnp.float32)
 
@@ -405,15 +433,41 @@
         steps(base, chunks, other_load, next_load, body, more)
 
     first_forward(last, 0)
-    first_end(last - 1, 0)
+    for g in range(len(GROUPS)):
+        first_end(last - 1, g)
+    first_r(2).start()
     first_end(last, 0)
-    r_begin(0)
+    first_r(3, 0).start()
     first_forward(last, 1)
     partner_gradient(0, blocks, other_load)
-    first_end(last - 1, 1)
     first_end(last, 1)
-    r_begin(1)
-    partner_gradient(1, blocks, own_load)
+    first_r(3, 1).start()
+    partner_gradient(1, blocks + chunks, own_load)
+
+    def first_r_pass(block, of, which, device):
+        lanes = pl.ds(pl.multiple_of(block * rows + of * piece, piece), piece)
+        return pltpu.make_async_remote_copy(
+            src_ref=ra.at[:, lanes], dst_ref=ra.at[:, lanes],
+            send_sem=p_send.at[block, which], recv_sem=p_recv.at[block, which], device_id=device, device_id_type=MESH)
+
+    def first_r_spread():
+        for block in range(3):
+            first_r(block).wait()
+        for g in range(len(GROUPS)):
+            first_r(3, g).wait()
+        for block in range(4):
+            first_r_pass(block, f, 0, near_id).start()
+            first_r_pass(block, f, 1, far_id).start()
+        for block in range(4):
+            first_r_pass(block, far, 1, far_id).wait_recv()
+        for block in range(4):
+            first_r_pass(block, far, 2, near_id).start()
+        for block in range(4):
+            first_r_pass(block, near, 0, near_id).wait_recv()
+            first_r_pass(block, far, 2, near_id).wait_recv()
+            first_r_pass(block, f, 0, near_id).wait_send()
+            first_r_pass(block, f, 1, far_id).wait_send()
+            first_r_pass(block, far, 2, near_id).wait_send()
 
     eta_load.wait()
     for k in range(ahead):
@@ -430,7 +484,7 @@
 
     lax.fori_loop(0, chunks, keep, 0)
     for_ship(lambda where: ship(where).wait())
-    r_spread(0)
+    first_r_spread()
 
     def w_store(ref, first, n, k):
         rows = pl.ds(pl.multiple_of(k * CHUNK, CHUNK), CHUNK)
@@ -474,9 +528,13 @@
     def sweep(t, carry):
         parity = (t + 1) % 2
         more = t < SWEEPS - 1
-        at = t * (6 * chunks + 2)
+        at = blocks + 2 * chunks + t * (6 * chunks + 2)
         own_columns(0, t, at, own_load)
-        r_spread(1)
+
+        @pl.when(t > 0)
+        def _():
+            r_spread(1)
+
         own_columns(1, t, at + chunks + 1, other_load)
 
         @pl.when(jnp.logical_not(more))
@@ -627,14 +685,14 @@
             out_specs=(in_hbm,) * (2 + len(sizes)),
             scratch_shapes=[
                 vmem((SLOTS, rows, CHUNK), bf16),
-                vmem((2, CHUNK, rows // ROW_BLOCKS), bf16),
+                vmem((2, CHUNK, rows // 4), bf16),
                 vmem((SLOTS + 2, CHUNK, width), f32),
                 vmem((chunks, width, CHUNK), f32),
                 vmem((chunks, width, CHUNK), f32),
                 vmem((2 * chunks, width, CHUNK), bf16),
                 vmem((chunks, width, CHUNK), f32),
                 vmem((width, rows), f32),
-                vmem((width, rows // ROW_BLOCKS), f32),
+                vmem((width, rows // 4), f32),
                 vmem((width, rows), f32),
                 vmem((width, rows), bf16),
                 vmem((width, rows), bf16),
@@ -642,18 +700,22 @@
                 vmem((columns // 128, 128), f32),
                 vmem((1, width), f32),
                 vmem((width, width), f32),
-                dma((SLOTS, ROW_BLOCKS)),
+                dma((SLOTS, max(count for _, count in BLOCKS))),
                 dma((SLOTS + 2,)),
                 dma((2,)),
                 dma((2,)),
+                dma((4 + groups - 1,)),
+                dma((4 + groups - 1,)),
+                dma((4, 3)),
+                dma((4, 3)),
                 dma((groups, 4)),
                 dma((groups, 4)),
                 dma((groups, chunks)),
                 dma((groups, chunks)),
                 dma((groups, chunks)),
                 dma((groups, chunks)),
-                dma((ROW_BLOCKS, groups, 3)),
-                dma((ROW_BLOCKS, groups, 3)),
+                dma((len(BLOCKS), groups, 3)),
+                dma((len(BLOCKS), groups, 3)),
                 dma((2, groups, 3)),
                 dma((2, groups, 3)),
                 dma((SLOTS,)),

time: 1300 us -> 1300 us (level)
  no operation moved by 1% of the time
where the time goes in v8:
time: 1300 us; the launch traced here: 1280 us
  Pallas kernels  1180 us (91%)
  waiting for transfers between devices  100 us (8%)
    pallas_call x1, Pallas kernels, local_sweeps(): pl.pallas_call(functools.partial(sweep_kernel, rows * samp_size), name='s...  1150 us
    ppermute x3, waiting for transfers between devices, local_sweeps(): arrived = [lax.ppermute(piece, 'samp', swap) for piece in pieces]  100 us
    pallas_call x7, Pallas kernels, place(): pl.pallas_call(body, name='place', out_shape=out_shape, grid_spec=pltpu.P...  30 us
  transfers between devices with their start and end apart: 3, of which 3 were waited for; matrix products, arithmetic and copies ran while one was open for 0% of the time, Pallas kernels for 2%

profile of v8, /device:TPU:0, one launch (start us, length us, event | category | flops | bytes accessed | tf_op | source)
XLA Modules:
  0.0 1284.8 jit_solution(10522911107011851054)
XLA Ops:
  0.6 1150.2 %sweeps.1 = (f32[2048,128]{1,0:T(8,128)}, bf16[2048,640]{1,0:T(8,128)(2,1)}, f32[4096,128]{1,0:T(8,128)}, f32[4096,128]{1,0:T(8,128)}, f32[6144,128]{1,0:T(8,128...) custom-call(bf16[2048,32768]{1,0:T(8,128)(2,1)} %x_hbm.1, f32[2048,128]{1,0:T(8,128)} %y_hbm.1, f32[32768,128]{1,0:T(8,128)} %w0_hbm.1, ...), custom_call_target="tpu_custom_call" | custom-call | tf_op jit(solution)/shard_map/sweeps/pallas_call | solution.py:676
  1150.8 0.5 collective-permute-start.2
  1151.4 1.5 collective-permute-start.1
  1152.9 0.5 collective-permute-start
  1153.4 4.5 place.7
  1157.9 5.3 place.8.other_ref
  1163.2 3.8 place.9.other_ref
  1166.9 4.7 place.10.other_ref
  1171.6 1.9 place.11.other_ref
  1173.5 42.9 %collective-permute-done.2.piece_ref = f32[6144,128]{1,0:T(8,128)} collective-permute-done((f32[6144,128]{1,0:T(8,128)}, f32[6144,128]{1,0:T(8,128)}, u32[]{:S(2)}, u32[]{:S(2)}) %collective-permute-start.2) | collective-permute-done | bytes 3145760 | tf_op jit(solution)/shard_map/ppermute | solution.py:731
  1216.4 5.3 place.12.other_ref
  1221.7 50.9 %collective-permute-done.1.piece_ref = f32[5120,128]{1,0:T(8,128)} collective-permute-done((f32[5120,128]{1,0:T(8,128)}, f32[5120,128]{1,0:T(8,128)}, u32[]{:S(2)}, u32[]{:S(2)}) %collective-permute-start.1) | collective-permute-done | bytes 2621472 | tf_op jit(solution)/shard_map/ppermute | solution.py:731
  1272.6 4.7 place.13.result_ref
  1277.3 6.6 collective-permute-done.piece_ref
  1283.8 0.8 place_last.1
Async XLA Ops:
  1150.8 65.6 %collective-permute-start.2 = (f32[6144,128]{1,0:T(8,128)}, f32[6144,128]{1,0:T(8,128)}, u32[]{:S(2)}, u32[]{:S(2)}) collective-permute-start(f32[6144,128]{1,0:T(8,128)} %get-tuple-element.12.piece_ref), channel_id=1, source_target_pairs={{0,4},{4,0},{1,5},{5,1},{2,6},{6,2},{3,7},{7,3}} | collective-permute-start | bytes 9437192 | tf_op jit(solution)/shard_map/ppermute | solution.py:731
  1151.4 121.2 %collective-permute-start.1 = (f32[5120,128]{1,0:T(8,128)}, f32[5120,128]{1,0:T(8,128)}, u32[]{:S(2)}, u32[]{:S(2)}) collective-permute-start(f32[5120,128]{1,0:T(8,128)} %get-tuple-element.11.piece_ref), channel_id=1, source_target_pairs={{0,4},{4,0},{1,5},{5,1},{2,6},{6,2},{3,7},{7,3}} | collective-permute-start | bytes 7864328 | tf_op jit(solution)/shard_map/ppermute | solution.py:731
  1152.9 130.9 %collective-permute-start = (f32[1024,128]{1,0:T(8,128)}, f32[1024,128]{1,0:T(8,128)S(1)}, u32[]{:S(2)}, u32[]{:S(2)}) collective-permute-start(f32[1024,128]{1,0:T(8,128)} %get-tuple-element.10.piece_ref), channel_id=1, source_target_pairs={{0,4},{4,0},{1,5},{5,1},{2,6},{6,2},{3,7},{7,3}} | collective-permute-start | bytes 1572872 | tf_op jit(solution)/shard_map/ppermute | solution.py:731
